TPU v7x, 128 devices: a whole 4x4x4 slice. The times are simulated.
128 devices in a mesh: frame: 64 (over x, z_lo, y, core), row: 2 (over z_hi).
Axes of the slice: x: 4, y: 4, z: 4 (z_hi: 2, z_lo: 2; z = z_hi * 2 + z_lo), core: 2. Of those that a mesh axis runs over, the one named last changes fastest.
Arguments:
- footage: float32 [256, 1024, 1024], P('frame', 'row'), may hold values from -30 to 30
Outputs:
- coefficients: float32 [256, 1024, 1024], P('frame', 'row')
- energies: float32 [4, 10], replicated
All inputs are finite; a program needn't handle non-finite values.
Results may differ from a plain program's by a relative error of at most 0.00007.
Values sent between devices are 32-bit elements; how exact they have to be, the bound alone decides.
A program may use at most 128 MiB of HBM per device.

v0:
```python
import jax
import jax.numpy as jnp
import numpy as np
from jax import lax
from jax.sharding import Mesh
from jax.sharding import PartitionSpec as P

SLEVELS = 3
TLEVELS = 3
FRAME = ("frame_0", "frame_1", "frame_2", "frame_3")
FRAME_ROW = ("frame_0", "frame_1", "frame_2", "frame_3", "row")


LIFT_ALPHA = -1.586134342
LIFT_BETA = -0.05298011854
LIFT_GAMMA = 0.8829110762
LIFT_DELTA = 0.4435068522
LIFT_ZETA = 1.149604398


def shifted(block, axis, distance):
    devices = range(lax.axis_size(axis))
    route = [(i - distance, i) for i in devices if i - distance in devices]
    return lax.ppermute(block, axis, route)


def over_axes(array, axes):
    for axis in axes:
        array = lax.psum(array, axis)
    return array


def mirror_after(values, along):
    length = values.shape[along]
    return jnp.concatenate(
        [
            lax.slice_in_dim(values, 1, length, axis=along),
            lax.slice_in_dim(values, length - 1, length, axis=along),
        ],
        axis=along,
    )


def mirror_before(values, along):
    length = values.shape[along]
    return jnp.concatenate(
        [
            lax.slice_in_dim(values, 0, 1, axis=along),
            lax.slice_in_dim(values, 0, length - 1, axis=along),
        ],
        axis=along,
    )


def weave_axis(even_part, odd_part, along):
    stacked = jnp.stack([even_part, odd_part], axis=along + 1)
    new_shape = list(even_part.shape)
    new_shape[along] = new_shape[along] * 2
    return stacked.reshape(tuple(new_shape))


def lift_pair(even_part, odd_part, take_next, take_prev):
    odd_part = odd_part + LIFT_ALPHA * (even_part + take_next(even_part))
    even_part = even_part + LIFT_BETA * (take_prev(odd_part) + odd_part)
    odd_part = odd_part + LIFT_GAMMA * (even_part + take_next(even_part))
    even_part = even_part + LIFT_DELTA * (take_prev(odd_part) + odd_part)
    return (even_part * LIFT_ZETA, odd_part * (1.0 / LIFT_ZETA))


def table_next(values):
    return np.concatenate([values[:, 1:], values[:, -1:]], axis=1)


def table_prev(values):
    return np.concatenate([values[:, :1], values[:, :-1]], axis=1)


def column_matrix(width):
    identity = np.eye(width)
    even_part = identity[:, 0::2]
    odd_part = identity[:, 1::2]
    odd_part = odd_part + LIFT_ALPHA * (even_part + table_next(even_part))
    even_part = even_part + LIFT_BETA * (table_prev(odd_part) + odd_part)
    odd_part = odd_part + LIFT_GAMMA * (even_part + table_next(even_part))
    even_part = even_part + LIFT_DELTA * (table_prev(odd_part) + odd_part)
    lifted = np.concatenate([even_part * LIFT_ZETA, odd_part * (1.0 / LIFT_ZETA)], axis=1)
    return jnp.asarray(lifted.astype(np.float32))


def spatial_inplace(block, levels):
    frame_count, row_count, width = block.shape
    mixed = jnp.dot(block, column_matrix(width), precision=lax.Precision.HIGHEST)
    paired = mixed.reshape(frame_count, row_count // 2, 2, width)
    low_rows, high_rows = lift_pair(paired[:, :, 0, :], paired[:, :, 1, :], rows_next, rows_prev)
    half_width = width // 2
    coarse = low_rows[..., :half_width]
    if levels > 1:
        coarse = spatial_inplace(coarse, levels - 1)
    upper_rows = weave_axis(coarse, low_rows[..., half_width:], 2)
    bottom = weave_axis(high_rows[..., :half_width], high_rows[..., half_width:], 2)
    return jnp.stack([upper_rows, bottom], axis=2).reshape(frame_count, row_count, width)


def temporal(planes_in, levels):
    even_part = planes_in[0::2]
    odd_part = planes_in[1::2]
    odd_part = odd_part - 0.5 * (even_part + mirror_after(even_part, 0))
    even_part = even_part + 0.25 * (mirror_before(odd_part, 0) + odd_part)
    if levels > 1:
        even_part = temporal(even_part, levels - 1)
    return weave_axis(even_part, odd_part, 0)


def rows_next(values):
    arrived = shifted(values[:, :1], "row", -1)
    is_last = lax.axis_index("row") == lax.axis_size("row") - 1
    return jnp.concatenate([values[:, 1:], jnp.where(is_last, values[:, -1:], arrived)], axis=1)


def rows_prev(values):
    arrived = shifted(values[:, -1:], "row", 1)
    is_first = lax.axis_index("row") == 0
    return jnp.concatenate([jnp.where(is_first, values[:, :1], arrived), values[:, :-1]], axis=1)


def level_of(number, ceiling):
    depth_now = 1
    while number % 2 == 0 and depth_now <= ceiling:
        number = number // 2
        depth_now = depth_now + 1
    return depth_now


def space_table(levels):
    period = 2**levels
    band_table = np.zeros((period * period, 3 * levels + 1), np.float32)
    for row_pos in range(period):
        for col_pos in range(period):
            row_level = level_of(row_pos, levels)
            col_level = level_of(col_pos, levels)
            finest = min(row_level, col_level)
            if finest > levels:
                column = 3 * levels
            elif row_level == col_level:
                column = 3 * (finest - 1) + 2
            elif row_level == finest:
                column = 3 * (finest - 1)
            else:
                column = 3 * (finest - 1) + 1
            band_table[row_pos * period + col_pos, column] = 1.0
    return band_table


def time_table(levels):
    period = 2**levels
    band_table = np.zeros((period, levels + 1), np.float32)
    for number in range(period):
        band_table[number, level_of(number, levels) - 1] = 1.0
    return band_table


def band_sums(coeffs, first_frame, levels_s, levels_t):
    period = 2**levels_s
    frame_count, row_count, col_count = coeffs.shape
    square = coeffs * coeffs
    row_folded = square.reshape(frame_count, row_count // period, period, col_count).sum(axis=1)
    column_phase = np.arange(col_count) % period
    selector = jnp.asarray((column_phase[:, None] == np.arange(period)[None, :]).astype(np.float32))
    pattern = jnp.dot(row_folded, selector, precision=lax.Precision.HIGHEST)
    pattern = pattern.reshape(frame_count, period * period)
    per_frame = jnp.dot(
        pattern, jnp.asarray(space_table(levels_s), jnp.float32), precision=lax.Precision.HIGHEST
    )
    time_period = 2**levels_t
    position = (first_frame + jnp.arange(frame_count, dtype=jnp.int32)) % time_period
    onehot = (position[:, None] == jnp.arange(time_period, dtype=jnp.int32)[None, :]).astype(
        jnp.float32
    )
    frame_band = jnp.dot(
        onehot, jnp.asarray(time_table(levels_t), jnp.float32), precision=lax.Precision.HIGHEST
    )
    return jnp.dot(frame_band.T, per_frame, precision=lax.Precision.HIGHEST)


def band_means(totals, frames_all, rows_all, cols_all, levels_s, levels_t):
    space_share = space_table(levels_s).sum(0) / float((2**levels_s) ** 2)
    time_share = time_table(levels_t).sum(0) / float(2**levels_t)
    counts = (
        float(frames_all) * float(rows_all) * float(cols_all) * np.outer(time_share, space_share)
    )
    return totals / jnp.asarray(counts, jnp.float32)


def shards(footage):
    frames_dev = footage.shape[0]
    planes = spatial_inplace(footage, SLEVELS)
    temporal_out = temporal(
        lax.all_to_all(planes, FRAME, split_axis=1, concat_axis=0, tiled=True), TLEVELS
    )
    coeffs = lax.all_to_all(temporal_out, FRAME, split_axis=0, concat_axis=1, tiled=True)
    totals = band_sums(coeffs, lax.axis_index(FRAME) * frames_dev, SLEVELS, TLEVELS)
    totals = over_axes(totals, FRAME_ROW)
    means = band_means(
        totals,
        frames_dev * lax.axis_size(FRAME),
        coeffs.shape[1] * lax.axis_size("row"),
        coeffs.shape[2],
        SLEVELS,
        TLEVELS,
    )
    return (coeffs, means)


def solution(mesh):
    finer = Mesh(
        mesh.devices.reshape(4, 2, 4, 2, mesh.shape["row"]),
        ("frame_0", "frame_1", "frame_2", "frame_3", "row"),
    )
    in_specs = (P(FRAME, "row", None),)
    out_specs = (P(FRAME, "row", None), P())
    return jax.shard_map(
        shards, mesh=finer, in_specs=in_specs, out_specs=out_specs, check_vma=False
    )
```

profile of v0, /device:TPU:1, one launch (start us, length us, event | category | flops | bytes accessed | tf_op | source)
XLA Modules:
  0.0 532.0 jit_solution(15202154321697548915)
XLA Ops:
  0.6 31.4 %convolution_bitcast_fusion = f32[4,512,1024]{2,1,0:T(8,128)} fusion(f32[1024,1024,1]{1,0,2:T(8,128)} %constant.100, f32[4,512,1024]{2,1,0:T(8,128)} %param.8), kind=kOutput, calls=%fused_computation.29 | convolution fusion | flops 25769803776 | bytes 20971520 | tf_op jit(solution)/shard_map/dot_general | solution.py:92
  32.0 10.6 %reshape.38 = f32[4,256,2,1024]{3,2,1,0:T(2,128)} reshape(f32[4,512,1024]{2,1,0:T(8,128)} %convolution_bitcast_fusion) | data formatting | bytes 16777216 | tf_op jit(solution)/shard_map/reshape | solution.py:93
  42.6 10.6 %fusion.50 = (f32[4,256,1,1024]{3,2,1,0:T(1,128)}, f32[4,256,1,1024]{3,2,1,0:T(1,128)S(1)}) fusion(f32[4,256,2,1024]{3,2,1,0:T(2,128)} %reshape.38), kind=kLoop, calls=%fused_computation.112 | loop fusion | bytes 16777216 | tf_op jit(solution)/shard_map/slice | solution.py:94
  57.3 2.5 slice.290
  59.8 2.3 collective-permute-done
  63.1 7.3 %fusion.1 = f32[4,256,1024]{2,1,0:T(8,128)S(1)} fusion(f32[4,1,1024]{2,1,0:T(1,128)S(1)} %broadcast_select_fusion.1, f32[4,255,1024]{2,1,0:T(8,128)} %slice.290, f32[4,256,1,1024]{3,2,1,0:T(1,128)} %get-tuple-element.8, f32[4,256,1,1024]{3,2,1,0:T(1,128)} %copy-done.2), kind=kLoop, calls=%fused_computation.7 | loop fusion | flops 4194304 | bytes 16777216 | tf_op jit(solution)/shard_map/add | solution.py:63
  70.4 2.0 copy-done
  72.4 4.3 collective-permute-start.1
  78.2 6.8 %fusion.3 = f32[4,256,1024]{2,1,0:T(8,128)S(1)} fusion(f32[4,256,1024]{2,1,0:T(8,128)} %copy-done, f32[4,255,1024]{2,1,0:T(8,128)} %bitcast.103, f32[4,1,1024]{2,1,0:T(1,128)S(1)} %broadcast_select_fusion.3, f32[4,256,1,1024]{3,2,1,0:T(1,128)} %copy-done.2), kind=kLoop, calls=%fused_computation.10 | loop fusion | flops 4194304 | bytes 16777216 | tf_op jit(solution)/shard_map/add | solution.py:64
  86.6 2.5 slice.296
  89.0 2.2 collective-permute-done.2
  91.3 5.8 %broadcast_multiply_fusion = (f32[4,256,1024]{2,1,0:T(8,128)}, f32[4,256,1024]{2,1,0:T(8,128)S(1)}) fusion(f32[4,256,1024]{2,1,0:T(8,128)S(1)} %copy-done.1, f32[4,256,1024]{2,1,0:T(8,128)S(1)} %fusion.3, f32[4,1,1024]{2,1,0:T(1,128)S(1)} %broadcast_select_fusion, f32[4,255,1024]{2,1,0:T(8,128)} %slice.296), kind=kLoop, calls=%fused_computation.43 | loop fusion | flops 5242880 | bytes 20971520 | tf_op jit(solution)/shard_map/mul | solution.py:67
  97.1 3.3 collective-permute-start.3
  102.9 2.0 copy-done.4
  104.9 4.8 fusion.13
  109.7 2.5 reshape.39
  115.6 4.5 collective-permute-done.4
  120.5 1.7 collective-permute-start.5
  124.6 2.5 pad_maximum_fusion.3
  127.1 5.4 %copy.49 = f32[4,256,512,2]{1,0,3,2:T(4,128)} copy(f32[4,256,512,2]{2,1,0,3:T(8,128)} %pad_maximum_fusion.3) | data formatting | bytes 8388608 | tf_op jit(solution)/shard_map/stack | solution.py:56
  133.1 14.5 %collective-permute-start.7 = (f32[4,1,512]{2,1,0:T(1,128)S(1)}, f32[4,1,512]{2,1,0:T(1,128)S(1)}, u32[]{:S(2)}, u32[]{:S(2)}) collective-permute-start(f32[4,1,512]{2,1,0:T(1,128)S(1)} %slice.315), channel_id=1, source_target_pairs={{0,1},{2,3},{4,5},{6,7},{8,9},{10,11},{12,13},{14,15},{16,17},{18,... | collective-permute-start | bytes 24584 | tf_op jit(solution)/shard_map/ppermute | solution.py:24
  155.5 9.1 %collective-permute-done.8 = f32[4,1,256]{1,2,0:T(8,128)S(1)} collective-permute-done((f32[4,1,256]{1,2,0:T(8,128)S(1)}, f32[4,1,256]{1,2,0:T(8,128)S(1)}, u32[]{:S(2)}, u32[]{:S(2)}) %collective-permute-start.8) | collective-permute-done | bytes 4128 | tf_op jit(solution)/shard_map/ppermute | solution.py:24
  166.1 2.1 collective-permute-start.9
  168.9 4.9 collective-permute-done.9
  176.4 9.9 %collective-permute-done.10 = f32[4,1,256]{1,2,0:T(8,128)S(1)} collective-permute-done((f32[4,1,256]{1,2,0:T(8,128)S(1)}, f32[4,1,256]{1,2,0:T(8,128)S(1)}, u32[]{:S(2)}, u32[]{:S(2)}) %collective-permute-start.10) | collective-permute-done | bytes 4128 | tf_op jit(solution)/shard_map/ppermute | solution.py:24
  189.1 5.4 %collective-permute-done.11 = f32[4,1,256]{1,2,0:T(8,128)S(1)} collective-permute-done((f32[4,1,256]{1,2,0:T(8,128)S(1)}, f32[4,1,256]{1,2,0:T(8,128)S(1)}, u32[]{:S(2)}, u32[]{:S(2)}) %collective-permute-start.11) | collective-permute-done | bytes 4128 | tf_op jit(solution)/shard_map/ppermute | solution.py:24
  200.8 2.4 copy.47
  203.2 3.9 stack_reshape.35
  207.0 4.2 pad_maximum_fusion.2
  211.3 5.5 %copy.48 = f32[4,256,512,2]{1,0,3,2:T(4,128)} copy(f32[4,256,512,2]{2,1,0,3:T(8,128)} %pad_maximum_fusion.2) | data formatting | bytes 8388608 | tf_op jit(solution)/shard_map/stack | solution.py:56
  216.8 8.8 %pad_maximum_fusion = f32[4,256,2,1024]{1,0,3,2:T(4,128)} fusion(f32[4,256,1,1024]{1,0,3,2:T(4,128)} %bitcast.115, f32[4,256,1,1024]{1,0,3,2:T(4,128)} %bitcast.116), kind=kLoop, calls=%fused_computation | loop fusion | flops 2097152 | bytes 16777216 | tf_op jit(solution)/shard_map/stack | solution.py:101
  225.6 11.4 %copy.50 = f32[4,256,2,1024]{3,0,2,1:T(4,128)} copy(f32[4,256,2,1024]{1,0,3,2:T(4,128)} %pad_maximum_fusion) | data formatting | bytes 16777216 | tf_op jit(solution)/shard_map/stack | solution.py:101
  237.1 112.8 %all_to_all.36 = f32[4,512,1024]{2,0,1:T(4,128)S(1)} all-to-all(f32[4,512,1024]{2,0,1:T(4,128)} %bitcast.107), channel_id=1, replica_groups=mesh['frame_0'=4,'frame_1'=2,'frame_2'=4,'frame_3'=2,'row'=2] {'frame_0'..., dimensions={1} | all-to-all | bytes 16777216 | tf_op jit(solution)/shard_map/all_to_all | solution.py:198
  349.9 4.9 copy.81
  354.7 1.7 copy.52
  357.5 2.0 fusion.10
  360.0 2.0 fusion.12
  367.4 1.7 pad_maximum_fusion.1
  369.1 4.2 copy.55
  373.3 6.6 %all-to-all-start.1 = ((f32[256,8,1024]{2,1,0:T(8,128)}), f32[256,8,1024]{2,1,0:T(8,128)}, u32[]{:S(2)}, u32[]{:S(2)}) async-start(f32[256,8,1024]{2,1,0:T(8,128)} %bitcast.106), calls=%async_computation.1 | async-start | bytes 16777216 | tf_op jit(solution)/shard_map/all_to_all | solution.py:200
  380.1 101.6 %all-to-all-done.1 = f32[256,8,1024]{2,1,0:T(8,128)} async-done(((f32[256,8,1024]{2,1,0:T(8,128)}), f32[256,8,1024]{2,1,0:T(8,128)}, u32[]{:S(2)}, u32[]{:S(2)}) %all-to-all-start.1) | async-done | bytes 8388640 | tf_op jit(solution)/shard_map/all_to_all | solution.py:200
  481.7 4.4 multiply_reduce_fusion
  486.8 7.7 %psum.35 = f32[4,10]{1,0:T(4,128)S(1)} all-reduce(f32[4,10]{1,0:T(4,128)S(1)} %fusion.56), channel_id=1, replica_groups=mesh['frame_0'=4,'frame_1'=2,'frame_2'=4,'frame_3'=2,'row'=2] {'frame_0'}, use_global_device_ids=true, to_apply=%region_1.2 | all-reduce | flops 40 | bytes 320 | tf_op jit(solution)/shard_map/psum | solution.py:29
  494.5 8.2 %psum.36 = f32[4,10]{1,0:T(4,128)S(1)} all-reduce(f32[4,10]{1,0:T(4,128)S(1)} %psum.35), channel_id=1, replica_groups=mesh['frame_0'=4,'frame_1'=2,'frame_2'=4,'frame_3'=2,'row'=2] {'frame_1'}, use_global_device_ids=true, to_apply=%region_2.3 | all-reduce | flops 40 | bytes 320 | tf_op jit(solution)/shard_map/psum | solution.py:29
  502.7 6.0 %psum.37 = f32[4,10]{1,0:T(4,128)S(1)} all-reduce(f32[4,10]{1,0:T(4,128)S(1)} %psum.36), channel_id=1, replica_groups=mesh['frame_0'=4,'frame_1'=2,'frame_2'=4,'frame_3'=2,'row'=2] {'frame_2'}, use_global_device_ids=true, to_apply=%region_3.4 | all-reduce | flops 40 | bytes 320 | tf_op jit(solution)/shard_map/psum | solution.py:29
  508.7 7.3 %psum.38 = f32[4,10]{1,0:T(4,128)S(1)} all-reduce(f32[4,10]{1,0:T(4,128)S(1)} %psum.37), channel_id=1, replica_groups=mesh['frame_0'=4,'frame_1'=2,'frame_2'=4,'frame_3'=2,'row'=2] {'frame_3'}, use_global_device_ids=true, to_apply=%region_4.5 | all-reduce | flops 40 | bytes 320 | tf_op jit(solution)/shard_map/psum | solution.py:29
  516.0 6.6 %psum.39 = f32[4,10]{1,0:T(4,128)S(1)} all-reduce(f32[4,10]{1,0:T(4,128)S(1)} %psum.38), channel_id=1, replica_groups=mesh['frame_0'=4,'frame_1'=2,'frame_2'=4,'frame_3'=2,'row'=2] {'row'}, use_global_device_ids=true, to_apply=%region_5.6 | all-reduce | flops 40 | bytes 320 | tf_op jit(solution)/shard_map/psum | solution.py:29
  523.2 8.4 %copy_bitcast_fusion = f32[4,512,1024]{2,1,0:T(8,128)} fusion(f32[256,8,1024]{2,1,0:T(8,128)} %all-to-all-done.1), kind=kLoop, calls=%fused_computation.2 | loop fusion | bytes 16777216 | tf_op jit(solution)/shard_map/all_to_all | solution.py:200
  (138 shorter events, 47.0 us)
Async XLA Ops:
  53.2 2.0 copy-start.2
  55.3 2.0 copy-start.3
  55.3 6.8 %collective-permute-start = (f32[4,1,1024]{2,1,0:T(1,128)S(1)}, f32[4,1,1024]{2,1,0:T(1,128)S(1)}, u32[]{:S(2)}, u32[]{:S(2)}) collective-permute-start(f32[4,1,1024]{2,1,0:T(1,128)S(1)} %slice.292), channel_id=1, source_target_pairs={{1,0},{3,2},{5,4},{7,6},{9,8},{11,10},{13,12},{15,14},{17,16},{19,... | collective-permute-start | bytes 49160 | tf_op jit(solution)/shard_map/ppermute | solution.py:24
  70.4 2.0 copy-start
  72.4 4.9 collective-permute-start.1
  85.0 6.3 %copy-start.1 = (f32[4,256,1024]{2,1,0:T(8,128)S(1)}, f32[4,256,1024]{2,1,0:T(8,128)}, u32[]{:S(2)}) copy-start(f32[4,256,1024]{2,1,0:T(8,128)} %copy-done) | copy-start | bytes 12582916
  85.0 6.3 %collective-permute-start.2 = (f32[4,1,1024]{2,1,0:T(1,128)S(1)}, f32[4,1,1024]{2,1,0:T(1,128)S(1)}, u32[]{:S(2)}, u32[]{:S(2)}) collective-permute-start(f32[4,1,1024]{2,1,0:T(1,128)S(1)} %slice.298), channel_id=1, source_target_pairs={{1,0},{3,2},{5,4},{7,6},{9,8},{11,10},{13,12},{15,14},{17,16},{19,... | collective-permute-start | bytes 49160 | tf_op jit(solution)/shard_map/ppermute | solution.py:24
  97.1 4.1 collective-permute-start.3
  101.3 3.6 copy-start.13
  102.9 2.0 copy-start.4
  113.8 8.4 %copy-start.6 = (f32[4,256,1024]{2,1,0:T(8,128)S(1)}, f32[4,256,1024]{2,1,0:T(8,128)}, u32[]{:S(2)}) copy-start(f32[4,256,1024]{2,1,0:T(8,128)} %get-tuple-element.6) | copy-start | bytes 12582916
  113.9 6.2 %collective-permute-start.4 = (f32[4,1,512]{2,1,0:T(1,128)S(1)}, f32[4,1,512]{2,1,0:T(1,128)S(1)}, u32[]{:S(2)}, u32[]{:S(2)}) collective-permute-start(f32[4,1,512]{2,1,0:T(1,128)S(1)} %slice.307), channel_id=1, source_target_pairs={{1,0},{3,2},{5,4},{7,6},{9,8},{11,10},{13,12},{15,14},{17,16},{19,... | collective-permute-start | bytes 24584 | tf_op jit(solution)/shard_map/ppermute | solution.py:24
  120.5 2.4 collective-permute-start.5
  123.3 9.3 %collective-permute-start.6 = (f32[4,1,512]{2,1,0:T(1,128)S(1)}, f32[4,1,512]{2,1,0:T(1,128)S(1)}, u32[]{:S(2)}, u32[]{:S(2)}) collective-permute-start(f32[4,1,512]{2,1,0:T(1,128)S(1)} %slice.313), channel_id=1, source_target_pairs={{1,0},{3,2},{5,4},{7,6},{9,8},{11,10},{13,12},{15,14},{17,16},{19,... | collective-permute-start | bytes 24584 | tf_op jit(solution)/shard_map/ppermute | solution.py:24
  132.5 15.1 %copy-start.5 = (f32[4,256,1024]{2,1,0:T(8,128)S(1)}, f32[4,256,1024]{2,1,0:T(8,128)}, u32[]{:S(2)}) copy-start(f32[4,256,1024]{2,1,0:T(8,128)} %copy-done.4) | copy-start | bytes 12582916
  133.1 16.4 %copy-start.14 = (f32[256,256,1]{1,0,2:T(8,128)S(1)}, f32[256,256,1]{1,0,2:T(8,128)}, u32[]{:S(2)}) copy-start(f32[256,256,1]{1,0,2:T(8,128)} %constant.102) | copy-start | bytes 786436
  133.1 16.0 %collective-permute-start.7 = (f32[4,1,512]{2,1,0:T(1,128)S(1)}, f32[4,1,512]{2,1,0:T(1,128)S(1)}, u32[]{:S(2)}, u32[]{:S(2)}) collective-permute-start(f32[4,1,512]{2,1,0:T(1,128)S(1)} %slice.315), channel_id=1, source_target_pairs={{0,1},{2,3},{4,5},{6,7},{8,9},{10,11},{12,13},{14,15},{16,17},{18,... | collective-permute-start | bytes 24584 | tf_op jit(solution)/shard_map/ppermute | solution.py:24
  149.5 15.3 %copy-start.8 = (f32[4,128,512]{2,1,0:T(8,128)}, f32[4,128,512]{2,1,0:T(8,128)S(1)}, u32[]{:S(2)}) copy-start(f32[4,128,512]{2,1,0:T(8,128)S(1)} %fusion.27) | copy-start | bytes 3145732
  152.7 11.9 %collective-permute-start.8 = (f32[4,1,256]{1,2,0:T(8,128)S(1)}, f32[4,1,256]{1,2,0:T(8,128)S(1)}, u32[]{:S(2)}, u32[]{:S(2)}) collective-permute-start(f32[4,1,256]{1,2,0:T(8,128)S(1)} %bitcast.120), channel_id=1, source_target_pairs={{1,0},{3,2},{5,4},{7,6},{9,8},{11,10},{13,12},{15,14},{17,16},{19,... | collective-permute-start | bytes 12296 | tf_op jit(solution)/shard_map/ppermute | solution.py:24
  155.5 12.7 %copy-start.11 = (f32[4,128,256,1]{2,1,0,3:T(8,128)S(1)}, f32[4,128,256,1]{2,1,0,3:T(8,128)}, u32[]{:S(2)}) copy-start(f32[4,128,256,1]{2,1,0,3:T(8,128)} %get-tuple-element.14) | copy-start | bytes 1572868
  155.5 12.7 %copy-start.12 = (f32[4,128,256,1]{2,1,0,3:T(8,128)S(1)}, f32[4,128,256,1]{2,1,0,3:T(8,128)}, u32[]{:S(2)}) copy-start(f32[4,128,256,1]{2,1,0,3:T(8,128)} %get-tuple-element.15) | copy-start | bytes 1572868
  166.1 7.7 %collective-permute-start.9 = (f32[4,1,256]{1,2,0:T(8,128)}, f32[4,1,256]{1,2,0:T(8,128)}, u32[]{:S(2)}, u32[]{:S(2)}) collective-permute-start(f32[4,1,256]{1,2,0:T(8,128)} %slice.324), channel_id=1, source_target_pairs={{0,1},{2,3},{4,5},{6,7},{8,9},{10,11},{12,13},{14,15},{16,17},{18,... | collective-permute-start | bytes 12296 | tf_op jit(solution)/shard_map/ppermute | solution.py:24
  168.9 6.5 %copy-start.9 = (f32[4,128,512]{2,1,0:T(8,128)S(1)}, f32[4,128,512]{2,1,0:T(8,128)}, u32[]{:S(2)}) copy-start(f32[4,128,512]{2,1,0:T(8,128)} %copy-done.8) | copy-start | bytes 3145732
  174.1 12.3 %collective-permute-start.10 = (f32[4,1,256]{1,2,0:T(8,128)S(1)}, f32[4,1,256]{1,2,0:T(8,128)S(1)}, u32[]{:S(2)}, u32[]{:S(2)}) collective-permute-start(f32[4,1,256]{1,2,0:T(8,128)S(1)} %bitcast.119), channel_id=1, source_target_pairs={{1,0},{3,2},{5,4},{7,6},{9,8},{11,10},{13,12},{15,14},{17,16},{19,... | collective-permute-start | bytes 12296 | tf_op jit(solution)/shard_map/ppermute | solution.py:24
  187.0 7.6 %collective-permute-start.11 = (f32[4,1,256]{1,2,0:T(8,128)S(1)}, f32[4,1,256]{1,2,0:T(8,128)S(1)}, u32[]{:S(2)}, u32[]{:S(2)}) collective-permute-start(f32[4,1,256]{1,2,0:T(8,128)S(1)} %slice.330), channel_id=1, source_target_pairs={{0,1},{2,3},{4,5},{6,7},{8,9},{10,11},{12,13},{14,15},{16,17},{18,... | collective-permute-start | bytes 12296 | tf_op jit(solution)/shard_map/ppermute | solution.py:24
  194.9 2.1 copy-start.10
  203.1 3.9 copy-start.7
  373.3 6.6 %copy-start.18 = (f32[8,4]{1,0:T(8,128)S(1)}, f32[8,4]{1,0:T(8,128)}, u32[]{:S(2)}) copy-start(f32[8,4]{1,0:T(8,128)} %constant.96.clone) | copy-start | bytes 388
  373.3 108.4 %all-to-all-start.1 = ((f32[256,8,1024]{2,1,0:T(8,128)}), f32[256,8,1024]{2,1,0:T(8,128)}, u32[]{:S(2)}, u32[]{:S(2)}) async-start(f32[256,8,1024]{2,1,0:T(8,128)} %bitcast.106), calls=%async_computation.1 | async-start | bytes 16777216 | tf_op jit(solution)/shard_map/all_to_all | solution.py:200
  481.7 4.4 copy-start.16
  481.7 4.7 copy-start.15
  481.7 40.8 %copy-start.17 = (f32[4,10]{1,0:T(4,128)S(1)}, f32[4,10]{1,0:T(4,128)}, u32[]{:S(2)}) copy-start(f32[4,10]{1,0:T(4,128)} %constant.99) | copy-start | bytes 484
where the time goes:
time: 542 us; the launch traced here: 532 us
  blocking collectives  149 us (27%)
  waiting for transfers between devices  142 us (26%)
  local copies, waits for them, and re-layouts  101 us (19%)
  other arithmetic  59.1 us (11%)
  starting transfers between devices  42.1 us (8%)
  matrix products  37.5 us (7%)
    all_to_all x1, blocking collectives, shards(): lax.all_to_all(planes, FRAME, split_axis=1, concat_axis=0, tiled=True)  113 us
    all_to_all x1, waiting for transfers between devices, shards(): lax.all_to_all(temporal_out, FRAME, split_axis=0, concat_axis=1, tiled=True)  102 us
    ppermute x12, waiting for transfers between devices, shifted(): return lax.ppermute(block, axis, route)  40.2 us
    dot_general x3, matrix products, spatial_inplace(): jnp.dot(block, column_matrix(width), precision=lax.Precision.HIGHEST)  36.7 us
    psum x5, blocking collectives, over_axes(): array = lax.psum(array, axis)  35.8 us
    ppermute x12, starting transfers between devices, shifted(): return lax.ppermute(block, axis, route)  35.6 us
    another operation x15, local copies, waits for them, and re-layouts, weave_axis(): stacked = jnp.stack([even_part, odd_part], axis=along + 1)  27.2 us
    another operation x3, local copies, waits for them, and re-layouts, spatial_inplace(): jnp.stack([upper_rows, bottom], axis=2)  14.1 us
  transfers between devices with their start and end apart: 13, of which 11 were waited for; matrix products, arithmetic and copies ran while one was open for 4% of the time, Pallas kernels for 0%

commit v1 on v0

v1 whole, which is shorter than its diff:
```python
import functools

import jax
import jax.numpy as jnp
import ml_dtypes
import numpy as np
from jax import lax
from jax.experimental import pallas as pl
from jax.experimental.pallas import tpu as pltpu
from jax.sharding import PartitionSpec as P

SLEVELS = 3
TLEVELS = 3
ALPHA = -1.586134342
BETA = -0.05298011854
GAMMA = 0.8829110762
DELTA = 0.4435068522
ZETA = 1.149604398
HALO = 32
PAD = 8
LANES = 128


def lift_matrix(width):
    x = np.eye(width)
    e, o = x[:, 0::2], x[:, 1::2]
    after = lambda v: np.concatenate([v[:, 1:], v[:, -1:]], axis=1)
    before = lambda v: np.concatenate([v[:, :1], v[:, :-1]], axis=1)
    o = o + ALPHA * (e + after(e))
    e = e + BETA * (before(o) + o)
    o = o + GAMMA * (e + after(e))
    e = e + DELTA * (before(o) + o)
    out = np.zeros((width, width))
    out[:, 0::2] = e * ZETA
    out[:, 1::2] = o * (1.0 / ZETA)
    return out


def weight_blocks(width):
    levels = []
    for level in range(SLEVELS):
        s = 2**level
        m = np.zeros((width, width))
        m[::s, ::s] = lift_matrix(width // s)
        b = LANES
        mid = width // 2
        blocks = np.stack([
            m[:b, :b],
            m[mid:mid + b, mid:mid + b],
            m[width - b:, width - b:],
            m[mid - b:mid, mid:mid + b],
            m[mid + b:mid + 2 * b, mid:mid + b],
        ])
        hi = blocks.astype(ml_dtypes.bfloat16)
        lo = (blocks - hi.astype(np.float64)).astype(ml_dtypes.bfloat16)
        levels.append(np.stack([hi, lo]))
    return np.stack(levels)


TILES = (
    ((0, 3), (4, 1), (None, 4), (None, None)),
    ((3, None), (1, 3), (4, 1), (None, 4)),
    ((None, None), (3, None), (1, 3), (4, 2)),
)


def build_weights(blocks_ref, w_ref):
    zero = jnp.zeros((LANES, LANES), jnp.bfloat16)

    def fill(index, carry):
        level, part = index // 2, index % 2
        for kind in range(3):
            for r in range(4):
                for c in range(2):
                    which = TILES[kind][r][c]
                    value = zero if which is None else blocks_ref[level, part, which]
                    w_ref[level, part, kind, r * LANES:(r + 1) * LANES, c * LANES:(c + 1) * LANES] = value
        return carry

    lax.fori_loop(0, SLEVELS * 2, fill, 0)


def columns(xs, w_ref, level, store):
    count = len(xs)
    his, los = [], []
    for x in xs:
        hi = x.astype(jnp.bfloat16)
        his.append(hi)
        los.append((x - hi.astype(jnp.float32)).astype(jnp.bfloat16))
    for tile in range(count // 2):
        if tile == 0:
            kind, start = 0, 0
        elif tile == count // 2 - 1:
            kind, start = 2, count - 4
        else:
            kind, start = 1, 2 * tile - 1
        hi = jnp.concatenate(his[start:start + 4], axis=1)
        lo = jnp.concatenate(los[start:start + 4], axis=1)
        whi = w_ref[level, 0, kind]
        wlo = w_ref[level, 1, kind]
        dot = functools.partial(jnp.dot, preferred_element_type=jnp.float32)
        acc = dot(hi, whi) + dot(lo, whi) + dot(hi, wlo)
        store(2 * tile, acc[:, :LANES])
        store(2 * tile + 1, acc[:, LANES:])


def lift_rows(buf, pairs):
    ev = pl.ds(PAD, pairs, stride=2)
    od = pl.ds(PAD + 1, pairs, stride=2)
    ev_next = pl.ds(PAD + 2, pairs, stride=2)
    od_prev = pl.ds(PAD - 1, pairs, stride=2)
    end = PAD + 2 * pairs

    def panel(p, carry):
        def mirror_end():
            buf[p, end:end + 1, :] = buf[p, end - 2:end - 1, :]

        def mirror_start():
            buf[p, PAD - 1:PAD, :] = buf[p, PAD + 1:PAD + 2, :]

        mirror_end()
        buf[p, od, :] = buf[p, od, :] * (1.0 / ZETA) + (ALPHA / ZETA) * (buf[p, ev, :] + buf[p, ev_next, :])
        mirror_start()
        buf[p, ev, :] = buf[p, ev, :] + (BETA * ZETA) * (buf[p, od_prev, :] + buf[p, od, :])
        mirror_end()
        buf[p, od, :] = buf[p, od, :] + (GAMMA / ZETA) * (buf[p, ev, :] + buf[p, ev_next, :])
        mirror_start()
        buf[p, ev, :] = buf[p, ev, :] * ZETA + (DELTA * ZETA * ZETA) * (buf[p, od_prev, :] + buf[p, od, :])
        return carry

    lax.fori_loop(0, buf.shape[0], panel, 0)


def spatial(own, halo, upper, w_ref, bufs, write):
    one, two, three = bufs
    panels = one.shape[0]
    rows = one.shape[1] - 2 * PAD
    strip = rows - HALO
    own_at = PAD + HALO * upper
    halo_at = PAD + strip * (1 - upper)
    half = strip // 2

    def store_top(p, value):
        one[p, pl.ds(pl.multiple_of(own_at, 8), half), :] = value

    def store_rest(p, value):
        one[p, pl.ds(pl.multiple_of(own_at + half, 8), half), :] = value[:half]
        one[p, pl.ds(pl.multiple_of(halo_at, 8), HALO), :] = value[half:]

    columns(own(0, half), w_ref, 0, store_top)
    rest = [jnp.concatenate(pair, axis=0) for pair in zip(own(half, half), halo())]
    columns(rest, w_ref, 0, store_rest)
    lift_rows(one, rows // 2)

    def into(buf, n):
        def store(p, value):
            buf[p, PAD:PAD + n, :] = value
        return store

    def evens(buf, n):
        return [buf[p, pl.ds(PAD, n, stride=2), :] for p in range(panels)]

    columns(evens(one, rows // 2), w_ref, 1, into(two, rows // 2))
    lift_rows(two, rows // 4)
    columns(evens(two, rows // 4), w_ref, 2, into(three, rows // 4))
    lift_rows(three, rows // 8)

    def merge(p, carry):
        lane = lax.broadcasted_iota(jnp.int32, (1, LANES), 1)
        n = rows // 4
        old = two[p, pl.ds(PAD, n, stride=2), :]
        two[p, pl.ds(PAD, n, stride=2), :] = jnp.where(lane % 4 == 0, three[p, PAD:PAD + n, :], old)
        n = rows // 2
        old = one[p, pl.ds(PAD, n, stride=2), :]
        one[p, pl.ds(PAD, n, stride=2), :] = jnp.where(lane % 2 == 0, two[p, PAD:PAD + n, :], old)
        return carry

    lax.fori_loop(0, panels, merge, 0)
    for p in range(panels):
        write(p, one[p, pl.ds(pl.multiple_of(own_at, 8), strip), :])


def level_of(number, ceiling):
    depth = 1
    while number % 2 == 0 and depth <= ceiling:
        number //= 2
        depth += 1
    return depth


def band_of(row, col):
    u, v = level_of(row, SLEVELS), level_of(col, SLEVELS)
    m = min(u, v)
    if m > SLEVELS:
        return 3 * SLEVELS
    if u == v:
        return 3 * (m - 1) + 2
    return 3 * (m - 1) + (0 if u == m else 1)


def position_level(pos):
    return jnp.where(pos % 2 == 1, 1, jnp.where(pos % 4 == 2, 2, jnp.where(pos % 8 == 4, 3, 4)))


def band_table(shape):
    u = position_level(lax.broadcasted_iota(jnp.int32, shape, 0))
    v = position_level(lax.broadcasted_iota(jnp.int32, shape, 1))
    m = jnp.minimum(u, v)
    kind = jnp.where(u == v, 2, jnp.where(u == m, 0, 1))
    return jnp.where(m == SLEVELS + 1, 3 * SLEVELS, 3 * (m - 1) + kind)


def spatial_kernel(own_ref, halo_ref, blocks_ref, out_ref, energy_ref, w_ref, one, two, three):
    plane = pl.program_id(0)
    upper = lax.axis_index("row")
    core = lax.axis_index("frame") % 2
    panels = one.shape[0]

    @pl.when(plane == 0)
    def _():
        build_weights(blocks_ref, w_ref)
        energy_ref[...] = jnp.zeros_like(energy_ref)

    def own(r, m):
        return [own_ref[0, r:r + m, p * LANES:(p + 1) * LANES] for p in range(panels)]

    def halo():
        return [halo_ref[0, :, p * LANES:(p + 1) * LANES] for p in range(panels)]

    squares = []

    def write(p, value):
        out_ref[0, :, p * LANES:(p + 1) * LANES] = value
        squares.append((value * value).reshape(-1, 8, LANES).sum(axis=0))

    spatial(own, halo, upper, w_ref, (one, two, three), write)
    total = functools.reduce(jnp.add, squares)
    time_band = jnp.where(plane == 0, jnp.where(core == 0, 3, 2), jnp.where(plane == 2, 1, 0))
    bands = band_table((8, LANES))
    row = lax.broadcasted_iota(jnp.int32, (8, LANES), 0)
    col = lax.broadcasted_iota(jnp.int32, (8, LANES), 1)
    acc = energy_ref[...]
    for s in range(3 * SLEVELS + 1):
        part = jnp.sum(jnp.where(bands == s, total, 0.0))
        acc = acc + jnp.where((row == time_band) & (col == s), part, 0.0)
    energy_ref[...] = acc


def spatial_call(planes, halos):
    n, strip, width = planes.shape
    panels = width // LANES
    rows = strip + HALO
    blocks = jnp.asarray(weight_blocks(width))
    scratch = lambda r: pltpu.VMEM((panels, r + 2 * PAD, LANES), jnp.float32)
    return pl.pallas_call(
        spatial_kernel,
        grid=(n,),
        out_shape=(
            jax.ShapeDtypeStruct((n, strip, width), jnp.float32),
            jax.ShapeDtypeStruct((8, LANES), jnp.float32),
        ),
        in_specs=[
            pl.BlockSpec((1, strip, width), lambda i: (i, 0, 0)),
            pl.BlockSpec((1, HALO, width), lambda i: (i, 0, 0)),
            pl.BlockSpec(memory_space=pltpu.VMEM),
        ],
        out_specs=(
            pl.BlockSpec((1, strip, width), lambda i: (i, 0, 0)),
            pl.BlockSpec((8, LANES), lambda i: (0, 0)),
        ),
        scratch_shapes=[
            pltpu.VMEM((SLEVELS, 2, 3, 4 * LANES, 2 * LANES), jnp.bfloat16),
            scratch(rows),
            scratch(rows // 2),
            scratch(rows // 4),
        ],
        compiler_params=pltpu.CompilerParams(vmem_limit_bytes=44 * 2**20),
        name="spatial",
    )(planes, halos, blocks)


def counts(frames, rows, cols):
    table = np.zeros(3 * SLEVELS + 1)
    for i in range(8):
        for j in range(8):
            table[band_of(i, j)] += 1 / 64
    share = np.array([0.5, 0.25, 0.125, 0.125])
    return float(frames) * rows * cols * np.outer(share, table)


def shards(footage):
    me = lax.axis_index("frame")
    devices = lax.axis_size("frame")
    first, last = me == 0, me == devices - 1
    odd = me % 2 == 1
    left = lambda x: lax.ppermute(x, "frame", [(i, i - 1) for i in range(1, devices)])
    right = lambda x: lax.ppermute(x, "frame", [(i, i + 1) for i in range(devices - 1)])
    f0, f1, f2, f3 = footage[0], footage[1], footage[2], footage[3]
    g = f3 - 0.5 * f2
    f4 = left(f0)
    g_prev = right(g)
    o1 = f1 - 0.5 * (f0 + f2)
    o3 = g - 0.5 * jnp.where(last, f2, f4)
    o_prev = jnp.where(first, o1, g_prev - 0.5 * f0)
    s0 = f0 + 0.25 * (o_prev + o1)
    s2 = f2 + 0.25 * (o1 + o3)
    h = s2 - 0.5 * s0
    s4 = left(s0)
    h_prev = right(h)
    d2 = h - 0.5 * jnp.where(last, s0, s4)
    d_prev = jnp.where(first, d2, h_prev - 0.5 * s0)
    t0 = s0 + 0.25 * (d_prev + d2)
    t_next = left(t0)
    t_prev = right(t0)
    p = t0 - 0.5 * t_prev
    high = p - 0.5 * jnp.where(last, t_prev, t_next)
    sent = jnp.where(odd, high, 0.0)
    hi_next = left(sent)
    hi_prev = right(sent)
    low = t0 + 0.25 * (jnp.where(first, hi_next, hi_prev) + hi_next)
    top = jnp.where(odd, high, low)
    coeffs = jnp.stack([top, o1, d2, o3])
    upper = lax.axis_index("row")
    strip = coeffs.shape[1]
    edge = jnp.where(upper == 0, coeffs[:, strip - HALO:], coeffs[:, :HALO])
    halos = lax.ppermute(edge, "row", [(0, 1), (1, 0)])
    out, energy = spatial_call(coeffs, halos)
    total = lax.psum(energy, ("frame", "row"))[:4, :3 * SLEVELS + 1]
    size = counts(4 * devices, strip * lax.axis_size("row"), footage.shape[2])
    return out, total / jnp.asarray(size, jnp.float32)


def solution(mesh):
    return jax.shard_map(
        shards,
        mesh=mesh,
        in_specs=(P("frame", "row", None),),
        out_specs=(P("frame", "row", None), P()),
        check_vma=False,
    )
```

time: 542 us -> 290 us (0.54); the launches traced: 532 us -> 290 us
  local copies, waits for them, and re-layouts: 101 us -> 0.03 us
  blocking collectives: 149 us -> 74.7 us
  matrix products: 37.5 us -> 0 us
  Pallas kernels: 0 us -> 28.4 us
  other arithmetic: 59.1 us -> 35.9 us
  waiting for transfers between devices: 142 us -> 123 us
  starting transfers between devices: 42.1 us -> 26.9 us
    all_to_all x1 -> x0, blocking collectives: 113 us -> none  [shards(): lax.all_to_all(planes, FRAME, split_axis=1, concat_axis=0, tiled=True)]
    all_to_all x1 -> x0, waiting for transfers between devices: 102 us -> none  [shards(): lax.all_to_all(temporal_out, FRAME, split_axis=0, concat_axis=1, tiled=True)]
    ppermute x12 -> x9, waiting for transfers between devices: 40.2 us -> 123 us  [the longest x4 60.4 us: shards(): lax.ppermute(x, 'frame', [(i, i + 1) for i in range(devices - 1)])]
    another operation x18 -> x0, local copies, waits for them, and re-layouts: 41.4 us -> none  [the longest x15 27.2 us: weave_axis(): stacked = jnp.stack([even_part, odd_part], axis=along + 1)]
    psum x5 -> x1, blocking collectives: 35.8 us -> 74.7 us  [shards(): total = lax.psum(energy, ('frame', 'row'))[:4, :3 * SLEVELS + 1]]
    dot_general x7 -> x0, matrix products: 37.5 us -> none  [the longest x3 36.7 us: spatial_inplace(): jnp.dot(block, column_matrix(width), precision=lax.Precision.HIGHEST)]
    pallas_call x0 -> x1, Pallas kernels: none -> 28.4 us  [spatial_call(): pl.pallas_call(spatial_kernel, grid=(n,), out_shape=(jax.ShapeDtypeStruct...]
    slice x35 -> x0, local copies, waits for them, and re-layouts: 22.9 us -> none  [the longest x3 13.3 us: spatial_inplace(): paired[:, :, 1, :]]
  transfers between devices with their start and end apart: 13 -> 9, of which waited for: 11 -> 9; matrix products, arithmetic and copies ran while one was open for 4% -> 4% of each run, Pallas kernels for 0% -> 0%
where the time goes in v1:
time: 290 us
  waiting for transfers between devices  123 us (42%)
  blocking collectives  74.7 us (26%)
  other arithmetic  35.9 us (12%)
  Pallas kernels  28.4 us (10%)
  starting transfers between devices  26.9 us (9%)
    psum x1, blocking collectives, shards(): total = lax.psum(energy, ('frame', 'row'))[:4, :3 * SLEVELS + 1]  74.7 us
    ppermute x4, waiting for transfers between devices, shards(): lax.ppermute(x, 'frame', [(i, i + 1) for i in range(devices - 1)])  60.4 us
    ppermute x4, waiting for transfers between devices, shards(): lax.ppermute(x, 'frame', [(i, i - 1) for i in range(1, devices)])  53.2 us
    pallas_call x1, Pallas kernels, spatial_call(): pl.pallas_call(spatial_kernel, grid=(n,), out_shape=(jax.ShapeDtypeStruct...  28.4 us
    ppermute x4, starting transfers between devices, shards(): lax.ppermute(x, 'frame', [(i, i + 1) for i in range(devices - 1)])  15.4 us
    another operation x3, other arithmetic, shards(): coeffs = jnp.stack([top, o1, d2, o3])  14.6 us
    ppermute x1, waiting for transfers between devices, shards(): halos = lax.ppermute(edge, 'row', [(0, 1), (1, 0)])  9.12 us
    ppermute x4, starting transfers between devices, shards(): lax.ppermute(x, 'frame', [(i, i - 1) for i in range(1, devices)])  7.67 us
  transfers between devices with their start and end apart: 9, of which 9 were waited for; matrix products, arithmetic and copies ran while one was open for 4% of the time, Pallas kernels for 0%

profile of v1, /device:TPU:1, one launch (start us, length us, event | category | flops | bytes accessed | tf_op | source)
XLA Modules:
  0.0 289.5 jit_solution(6384278184781226327)
XLA Ops:
  0.6 2.7 bitcast_subtract_fusion
  3.3 4.6 %collective-permute-start = (f32[512,1024]{1,0:T(8,128)S(1)}, f32[512,1024]{1,0:T(8,128)}, u32[]{:S(2)}, u32[]{:S(2)}) collective-permute-start(f32[512,1024]{1,0:T(8,128)S(1)} %bitcast_subtract_fusion), channel_id=1, source_target_pairs={{0,2},{2,4},{4,6},{6,8},{8,10},{10,12},{12,14},{14,16},{16,18},{18... | collective-permute-start | bytes 6291464 | tf_op jit(solution)/shard_map/ppermute | solution.py:297
  7.9 6.0 %multiply_subtract_fusion = (f32[1,512,1024]{2,1,0:T(8,128)}, f32[512,1024]{1,0:T(8,128)}) fusion(f32[4,512,1024]{2,1,0:T(8,128)} %param.3), kind=kLoop, calls=%fused_computation.22 | loop fusion | flops 1572864 | bytes 10485760 | tf_op jit(solution)/shard_map/sub | solution.py:302
  13.9 1.9 collective-permute-start.1
  15.8 15.0 %collective-permute-done = f32[512,1024]{1,0:T(8,128)} collective-permute-done((f32[512,1024]{1,0:T(8,128)S(1)}, f32[512,1024]{1,0:T(8,128)}, u32[]{:S(2)}, u32[]{:S(2)}) %collective-permute-start) | collective-permute-done | bytes 2097184 | tf_op jit(solution)/shard_map/ppermute | solution.py:297
  30.8 4.5 %fusion.1 = f32[512,1024]{1,0:T(8,128)S(1)} fusion(f32[512,1024]{1,0:T(8,128)} %collective-permute-done, f32[4,512,1024]{2,1,0:T(8,128)} %param.3, pred[]{:T(512)S(6)} %eq.15), kind=kLoop, calls=%fused_computation.5 | loop fusion | flops 4718592 | bytes 10485761 | tf_op jit(solution)/shard_map/add | solution.py:305
  35.3 0.0 copy-start.1
  35.3 1.9 collective-permute-start.2
  37.3 4.3 %collective-permute-done.1 = f32[512,1024]{1,0:T(8,128)} collective-permute-done((f32[512,1024]{1,0:T(8,128)}, f32[512,1024]{1,0:T(8,128)}, u32[]{:S(2)}, u32[]{:S(2)}) %collective-permute-start.1) | collective-permute-done | bytes 2097184 | tf_op jit(solution)/shard_map/ppermute | solution.py:296
  41.5 22.5 %collective-permute-done.2 = f32[512,1024]{1,0:T(8,128)} collective-permute-done((f32[512,1024]{1,0:T(8,128)S(1)}, f32[512,1024]{1,0:T(8,128)}, u32[]{:S(2)}, u32[]{:S(2)}) %collective-permute-start.2) | collective-permute-done | bytes 2097184 | tf_op jit(solution)/shard_map/ppermute | solution.py:296
  64.0 8.7 %fusion.13 = (f32[1,512,1024]{2,1,0:T(8,128)}, f32[512,1024]{1,0:T(8,128)S(1)}, f32[512,1024]{1,0:T(8,128)}) fusion(f32[512,1024]{1,0:T(8,128)S(1)} %fusion.1, f32[512,1024]{1,0:T(8,128)} %collective-permute-done.2, pred[]{:T(512)S(6)} %eq.16, f32[4,512,1024]{2,1,0:T(8,128)} %param.3, f32[512,1024]{1,0:T(8,128)} %collective-permute-done.1), kind=kLoop, calls=%fused_computation.27 | loop fusion | flops 8388608 | bytes 20971520 | tf_op jit(solution)/shard_map/stack | solution.py:322
  72.7 0.0 copy-done.1
  72.7 1.9 collective-permute-start.3
  74.6 23.0 %collective-permute-done.3 = f32[512,1024]{1,0:T(8,128)S(1)} collective-permute-done((f32[512,1024]{1,0:T(8,128)S(1)}, f32[512,1024]{1,0:T(8,128)S(1)}, u32[]{:S(2)}, u32[]{:S(2)}) %collective-permute-start.3) | collective-permute-done | bytes 2097184 | tf_op jit(solution)/shard_map/ppermute | solution.py:297
  97.6 3.2 %fusion.3 = f32[512,1024]{1,0:T(8,128)S(1)} fusion(f32[512,1024]{1,0:T(8,128)} %copy-done.1, f32[512,1024]{1,0:T(8,128)S(1)} %collective-permute-done.3, pred[]{:T(512)S(6)} %eq.15, f32[512,1024]{1,0:T(8,128)S(1)} %get-tuple-element.7, f32[512,1024]{1,0:T(8,128)} %collective-permute-done.2, pred[]{:T(512)S(6)} %eq.16), kind=kLoop, calls=%fused_computation.7 | loop fusion | flops 4718592 | bytes 10485762 | tf_op jit(solution)/shard_map/add | solution.py:312
  100.8 1.9 collective-permute-start.5
  102.7 4.4 %collective-permute-start.4 = (f32[512,1024]{1,0:T(8,128)S(1)}, f32[512,1024]{1,0:T(8,128)}, u32[]{:S(2)}, u32[]{:S(2)}) collective-permute-start(f32[512,1024]{1,0:T(8,128)S(1)} %fusion.3), channel_id=1, source_target_pairs={{0,2},{2,4},{4,6},{6,8},{8,10},{10,12},{12,14},{14,16},{16,18},{18... | collective-permute-start | bytes 6291464 | tf_op jit(solution)/shard_map/ppermute | solution.py:297
  107.1 21.9 %collective-permute-done.5 = f32[512,1024]{1,0:T(8,128)} collective-permute-done((f32[512,1024]{1,0:T(8,128)S(1)}, f32[512,1024]{1,0:T(8,128)}, u32[]{:S(2)}, u32[]{:S(2)}) %collective-permute-start.5) | collective-permute-done | bytes 2097184 | tf_op jit(solution)/shard_map/ppermute | solution.py:296
  129.0 1.1 collective-permute-done.4
  130.1 4.3 %broadcast_select_fusion = f32[512,1024]{1,0:T(8,128)} fusion(pred[]{:T(512)S(6)} %eq.14, f32[512,1024]{1,0:T(8,128)} %collective-permute-done.4, f32[512,1024]{1,0:T(8,128)} %collective-permute-done.5, pred[]{:T(512)S(6)} %eq.16, f32[512,1024]{1,0:T(8,128)S(1)} %fusion.3), kind=kLoop, calls=%fused_computation.26 | loop fusion | flops 3145728 | bytes 8388610 | tf_op jit(solution)/shard_map/jit(_where)/select_n | solution.py:317
  134.4 4.5 %collective-permute-start.7 = (f32[512,1024]{1,0:T(8,128)}, f32[512,1024]{1,0:T(8,128)}, u32[]{:S(2)}, u32[]{:S(2)}) collective-permute-start(f32[512,1024]{1,0:T(8,128)} %broadcast_select_fusion), channel_id=1, source_target_pairs={{0,2},{2,4},{4,6},{6,8},{8,10},{10,12},{12,14},{14,16},{16,18},{18... | collective-permute-start | bytes 6291464 | tf_op jit(solution)/shard_map/ppermute | solution.py:297
  138.9 1.9 collective-permute-start.6
  140.8 0.0 copy-start.2
  140.8 0.0 copy-start.3
  140.8 0.0 copy-start.4
  140.8 21.3 %collective-permute-done.7 = f32[512,1024]{1,0:T(8,128)} collective-permute-done((f32[512,1024]{1,0:T(8,128)}, f32[512,1024]{1,0:T(8,128)}, u32[]{:S(2)}, u32[]{:S(2)}) %collective-permute-start.7) | collective-permute-done | bytes 2097184 | tf_op jit(solution)/shard_map/ppermute | solution.py:297
  162.1 4.6 %collective-permute-done.6 = f32[512,1024]{1,0:T(8,128)} collective-permute-done((f32[512,1024]{1,0:T(8,128)}, f32[512,1024]{1,0:T(8,128)}, u32[]{:S(2)}, u32[]{:S(2)}) %collective-permute-start.6) | collective-permute-done | bytes 2097184 | tf_op jit(solution)/shard_map/ppermute | solution.py:296
  166.7 4.8 %fusion.7 = f32[1,512,1024]{2,1,0:T(8,128)S(1)} fusion(f32[512,1024]{1,0:T(8,128)S(1)} %fusion.3, f32[512,1024]{1,0:T(8,128)} %collective-permute-done.6, f32[512,1024]{1,0:T(8,128)} %collective-permute-done.7, pred[]{:T(512)S(6)} %eq.15, pred[]{:T(512)S(6)} %eq.14, f32[512,1024]{1,0:T(8,128)} %collective-permute-done.4, ...), kind=kLoop, calls=%fused_computation.11 | loop fusion | flops 5242880 | bytes 12582915 | tf_op jit(solution)/shard_map/stack | solution.py:322
  171.5 0.0 copy-done.2
  171.5 0.0 copy-done.3
  171.5 0.0 copy-done.4
  171.5 1.2 pad_maximum_fusion.own_ref
  172.7 0.0 copy-start
  172.7 0.1 slice_select_fusion
  172.8 0.0 copy-start.5
  172.8 3.9 %collective-permute-start.8 = (f32[4,32,1024]{2,1,0:T(8,128)S(1)}, f32[4,32,1024]{2,1,0:T(8,128)S(1)}, u32[]{:S(2)}, u32[]{:S(2)}) collective-permute-start(f32[4,32,1024]{2,1,0:T(8,128)S(1)} %slice_select_fusion), channel_id=1, source_target_pairs={{0,1},{1,0},{2,3},{3,2},{4,5},{5,4},{6,7},{7,6},{8,9},{9,8},{10,11... | collective-permute-start | bytes 1572872 | tf_op jit(solution)/shard_map/ppermute | solution.py:326
  176.7 9.1 %collective-permute-done.8.halo_ref = f32[4,32,1024]{2,1,0:T(8,128)S(1)} collective-permute-done((f32[4,32,1024]{2,1,0:T(8,128)S(1)}, f32[4,32,1024]{2,1,0:T(8,128)S(1)}, u32[]{:S(2)}, u32[]{:S(2)}) %collective-permute-start.8) | collective-permute-done | bytes 524320 | tf_op jit(solution)/shard_map/ppermute | solution.py:326
  185.8 0.0 copy-done
  185.8 28.4 %spatial.1 = (f32[4,512,1024]{2,1,0:T(8,128)}, f32[8,128]{1,0:T(8,128)S(1)}) custom-call(f32[4,512,1024]{2,1,0:T(8,128)S(1)} %pad_maximum_fusion.own_ref, f32[4,32,1024]{2,1,0:T(8,128)S(1)} %collective-permute-done.8.halo_ref, bf16[3,2,5,128,128]{4,3,2,1,0:T(8,128)(2,1)S(1)} %copy-done), custom_call_target="tpu_custom_call" | custom-call | tf_op jit(solution)/shard_map/spatial/pallas_call | solution.py:255
  214.2 74.7 %psum.7 = f32[8,128]{1,0:T(8,128)S(1)} all-reduce(f32[8,128]{1,0:T(8,128)S(1)} %get-tuple-element.5), channel_id=1, replica_groups=mesh['frame'=64,'row'=2] {'frame','row'}, use_global_device_ids=true, to_apply=%region_0.1 | all-reduce | flops 1024 | bytes 8192 | tf_op jit(solution)/shard_map/psum | solution.py:328
  288.9 0.0 copy-done.5
  288.9 0.6 slice_multiply_fusion
Async XLA Ops:
  3.3 27.5 %collective-permute-start = (f32[512,1024]{1,0:T(8,128)S(1)}, f32[512,1024]{1,0:T(8,128)}, u32[]{:S(2)}, u32[]{:S(2)}) collective-permute-start(f32[512,1024]{1,0:T(8,128)S(1)} %bitcast_subtract_fusion), channel_id=1, source_target_pairs={{0,2},{2,4},{4,6},{6,8},{8,10},{10,12},{12,14},{14,16},{16,18},{18... | collective-permute-start | bytes 6291464 | tf_op jit(solution)/shard_map/ppermute | solution.py:297
  13.9 27.7 %collective-permute-start.1 = (f32[512,1024]{1,0:T(8,128)}, f32[512,1024]{1,0:T(8,128)}, u32[]{:S(2)}, u32[]{:S(2)}) collective-permute-start(f32[512,1024]{1,0:T(8,128)} %get-tuple-element.10), channel_id=1, source_target_pairs={{2,0},{4,2},{6,4},{8,6},{10,8},{12,10},{14,12},{16,14},{18,16},{20... | collective-permute-start | bytes 6291464 | tf_op jit(solution)/shard_map/ppermute | solution.py:296
  35.3 37.4 %copy-start.1 = (f32[512,1024]{1,0:T(8,128)}, f32[512,1024]{1,0:T(8,128)S(1)}, u32[]{:S(2)}) copy-start(f32[512,1024]{1,0:T(8,128)S(1)} %fusion.1) | copy-start | bytes 6291460
  35.3 28.7 %collective-permute-start.2 = (f32[512,1024]{1,0:T(8,128)S(1)}, f32[512,1024]{1,0:T(8,128)}, u32[]{:S(2)}, u32[]{:S(2)}) collective-permute-start(f32[512,1024]{1,0:T(8,128)S(1)} %fusion.1), channel_id=1, source_target_pairs={{2,0},{4,2},{6,4},{8,6},{10,8},{12,10},{14,12},{16,14},{18,16},{20... | collective-permute-start | bytes 6291464 | tf_op jit(solution)/shard_map/ppermute | solution.py:296
  72.7 24.9 %collective-permute-start.3 = (f32[512,1024]{1,0:T(8,128)S(1)}, f32[512,1024]{1,0:T(8,128)S(1)}, u32[]{:S(2)}, u32[]{:S(2)}) collective-permute-start(f32[512,1024]{1,0:T(8,128)S(1)} %get-tuple-element.7), channel_id=1, source_target_pairs={{0,2},{2,4},{4,6},{6,8},{8,10},{10,12},{12,14},{14,16},{16,18},{18... | collective-permute-start | bytes 6291464 | tf_op jit(solution)/shard_map/ppermute | solution.py:297
  100.8 28.2 %collective-permute-start.5 = (f32[512,1024]{1,0:T(8,128)S(1)}, f32[512,1024]{1,0:T(8,128)}, u32[]{:S(2)}, u32[]{:S(2)}) collective-permute-start(f32[512,1024]{1,0:T(8,128)S(1)} %fusion.3), channel_id=1, source_target_pairs={{2,0},{4,2},{6,4},{8,6},{10,8},{12,10},{14,12},{16,14},{18,16},{20... | collective-permute-start | bytes 6291464 | tf_op jit(solution)/shard_map/ppermute | solution.py:296
  102.7 27.4 %collective-permute-start.4 = (f32[512,1024]{1,0:T(8,128)S(1)}, f32[512,1024]{1,0:T(8,128)}, u32[]{:S(2)}, u32[]{:S(2)}) collective-permute-start(f32[512,1024]{1,0:T(8,128)S(1)} %fusion.3), channel_id=1, source_target_pairs={{0,2},{2,4},{4,6},{6,8},{8,10},{10,12},{12,14},{14,16},{16,18},{18... | collective-permute-start | bytes 6291464 | tf_op jit(solution)/shard_map/ppermute | solution.py:297
  134.4 27.8 %collective-permute-start.7 = (f32[512,1024]{1,0:T(8,128)}, f32[512,1024]{1,0:T(8,128)}, u32[]{:S(2)}, u32[]{:S(2)}) collective-permute-start(f32[512,1024]{1,0:T(8,128)} %broadcast_select_fusion), channel_id=1, source_target_pairs={{0,2},{2,4},{4,6},{6,8},{8,10},{10,12},{12,14},{14,16},{16,18},{18... | collective-permute-start | bytes 6291464 | tf_op jit(solution)/shard_map/ppermute | solution.py:297
  138.9 27.9 %collective-permute-start.6 = (f32[512,1024]{1,0:T(8,128)}, f32[512,1024]{1,0:T(8,128)}, u32[]{:S(2)}, u32[]{:S(2)}) collective-permute-start(f32[512,1024]{1,0:T(8,128)} %broadcast_select_fusion), channel_id=1, source_target_pairs={{2,0},{4,2},{6,4},{8,6},{10,8},{12,10},{14,12},{16,14},{18,16},{20... | collective-permute-start | bytes 6291464 | tf_op jit(solution)/shard_map/ppermute | solution.py:296
  140.8 30.7 %copy-start.2 = (f32[1,512,1024]{2,1,0:T(8,128)S(1)}, f32[1,512,1024]{2,1,0:T(8,128)}, u32[]{:S(2)}) copy-start(f32[1,512,1024]{2,1,0:T(8,128)} %get-tuple-element.9) | copy-start | bytes 6291460
  140.8 30.7 %copy-start.3 = (f32[1,512,1024]{2,1,0:T(8,128)S(1)}, f32[1,512,1024]{2,1,0:T(8,128)}, u32[]{:S(2)}) copy-start(f32[1,512,1024]{2,1,0:T(8,128)} %get-tuple-element.6) | copy-start | bytes 6291460
  140.8 30.7 %copy-start.4 = (f32[512,1024]{1,0:T(8,128)S(1)}, f32[512,1024]{1,0:T(8,128)}, u32[]{:S(2)}) copy-start(f32[512,1024]{1,0:T(8,128)} %get-tuple-element.8) | copy-start | bytes 6291460
  172.7 13.1 %copy-start = (bf16[3,2,5,128,128]{4,3,2,1,0:T(8,128)(2,1)S(1)}, bf16[3,2,5,128,128]{4,3,2,1,0:T(8,128)(2,1)}, u32[]{:S(2)}) copy-start(bf16[3,2,5,128,128]{4,3,2,1,0:T(8,128)(2,1)} %constant.35.clone.blocks_ref) | copy-start | bytes 2949124
  172.8 116.1 %copy-start.5 = (f32[4,10]{1,0:T(4,128)S(1)}, f32[4,10]{1,0:T(4,128)}, u32[]{:S(2)}) copy-start(f32[4,10]{1,0:T(4,128)} %constant.38) | copy-start | bytes 484
  172.8 13.0 %collective-permute-start.8 = (f32[4,32,1024]{2,1,0:T(8,128)S(1)}, f32[4,32,1024]{2,1,0:T(8,128)S(1)}, u32[]{:S(2)}, u32[]{:S(2)}) collective-permute-start(f32[4,32,1024]{2,1,0:T(8,128)S(1)} %slice_select_fusion), channel_id=1, source_target_pairs={{0,1},{1,0},{2,3},{3,2},{4,5},{5,4},{6,7},{7,6},{8,9},{9,8},{10,11... | collective-permute-start | bytes 1572872 | tf_op jit(solution)/shard_map/ppermute | solution.py:326

commit v2 on v1

--- a/solution.py
+++ b/solution.py
@@ -19,6 +19,7 @@
 HALO = 32
 PAD = 8
 LANES = 128
+CHUNKS = 8
 
 
 def lift_matrix(width):
@@ -131,25 +132,30 @@
     lax.fori_loop(0, buf.shape[0], panel, 0)
 
 
-def spatial(own, halo, upper, w_ref, bufs, write):
+def spatial(own, halo, upper, w_ref, bufs, before=None, midway=None):
     one, two, three = bufs
     panels = one.shape[0]
     rows = one.shape[1] - 2 * PAD
     strip = rows - HALO
-    own_at = PAD + HALO * upper
-    halo_at = PAD + strip * (1 - upper)
     half = strip // 2
+    own_at = pl.multiple_of(PAD + HALO * upper, 8)
+    rest_at = pl.multiple_of(PAD + HALO * upper + half, 8)
+    halo_at = pl.multiple_of(PAD + strip * (1 - upper), 8)
 
     def store_top(p, value):
-        one[p, pl.ds(pl.multiple_of(own_at, 8), half), :] = value
+        one[p, pl.ds(own_at, half), :] = value
 
     def store_rest(p, value):
-        one[p, pl.ds(pl.multiple_of(own_at + half, 8), half), :] = value[:half]
-        one[p, pl.ds(pl.multiple_of(halo_at, 8), HALO), :] = value[half:]
-
+        one[p, pl.ds(rest_at, half), :] = value[:half]
+        one[p, pl.ds(halo_at, HALO), :] = value[half:]
+
+    if before is not None:
+        before()
     columns(own(0, half), w_ref, 0, store_top)
     rest = [jnp.concatenate(pair, axis=0) for pair in zip(own(half, half), halo())]
     columns(rest, w_ref, 0, store_rest)
+    if midway is not None:
+        midway()
     lift_rows(one, rows // 2)
 
     def into(buf, n):
@@ -176,8 +182,7 @@
         return carry
 
     lax.fori_loop(0, panels, merge, 0)
-    for p in range(panels):
-        write(p, one[p, pl.ds(pl.multiple_of(own_at, 8), strip), :])
+    return own_at
 
 
 def level_of(number, ceiling):
@@ -210,75 +215,6 @@
     return jnp.where(m == SLEVELS + 1, 3 * SLEVELS, 3 * (m - 1) + kind)
 
 
-def spatial_kernel(own_ref, halo_ref, blocks_ref, out_ref, energy_ref, w_ref, one, two, three):
-    plane = pl.program_id(0)
-    upper = lax.axis_index("row")
-    core = lax.axis_index("frame") % 2
-    panels = one.shape[0]
-
-    @pl.when(plane == 0)
-    def _():
-        build_weights(blocks_ref, w_ref)
-        energy_ref[...] = jnp.zeros_like(energy_ref)
-
-    def own(r, m):
-        return [own_ref[0, r:r + m, p * LANES:(p + 1) * LANES] for p in range(panels)]
-
-    def halo():
-        return [halo_ref[0, :, p * LANES:(p + 1) * LANES] for p in range(panels)]
-
-    squares = []
-
-    def write(p, value):
-        out_ref[0, :, p * LANES:(p + 1) * LANES] = value
-        squares.append((value * value).reshape(-1, 8, LANES).sum(axis=0))
-
-    spatial(own, halo, upper, w_ref, (one, two, three), write)
-    total = functools.reduce(jnp.add, squares)
-    time_band = jnp.where(plane == 0, jnp.where(core == 0, 3, 2), jnp.where(plane == 2, 1, 0))
-    bands = band_table((8, LANES))
-    row = lax.broadcasted_iota(jnp.int32, (8, LANES), 0)
-    col = lax.broadcasted_iota(jnp.int32, (8, LANES), 1)
-    acc = energy_ref[...]
-    for s in range(3 * SLEVELS + 1):
-        part = jnp.sum(jnp.where(bands == s, total, 0.0))
-        acc = acc + jnp.where((row == time_band) & (col == s), part, 0.0)
-    energy_ref[...] = acc
-
-
-def spatial_call(planes, halos):
-    n, strip, width = planes.shape
-    panels = width // LANES
-    rows = strip + HALO
-    blocks = jnp.asarray(weight_blocks(width))
-    scratch = lambda r: pltpu.VMEM((panels, r + 2 * PAD, LANES), jnp.float32)
-    return pl.pallas_call(
-        spatial_kernel,
-        grid=(n,),
-        out_shape=(
-            jax.ShapeDtypeStruct((n, strip, width), jnp.float32),
-            jax.ShapeDtypeStruct((8, LANES), jnp.float32),
-        ),
-        in_specs=[
-            pl.BlockSpec((1, strip, width), lambda i: (i, 0, 0)),
-            pl.BlockSpec((1, HALO, width), lambda i: (i, 0, 0)),
-            pl.BlockSpec(memory_space=pltpu.VMEM),
-        ],
-        out_specs=(
-            pl.BlockSpec((1, strip, width), lambda i: (i, 0, 0)),
-            pl.BlockSpec((8, LANES), lambda i: (0, 0)),
-        ),
-        scratch_shapes=[
-            pltpu.VMEM((SLEVELS, 2, 3, 4 * LANES, 2 * LANES), jnp.bfloat16),
-            scratch(rows),
-            scratch(rows // 2),
-            scratch(rows // 4),
-        ],
-        compiler_params=pltpu.CompilerParams(vmem_limit_bytes=44 * 2**20),
-        name="spatial",
-    )(planes, halos, blocks)
-
-
 def counts(frames, rows, cols):
     table = np.zeros(3 * SLEVELS + 1)
     for i in range(8):
@@ -288,46 +224,315 @@
     return float(frames) * rows * cols * np.outer(share, table)
 
 
+def band_energy(one, at, strip, time_band):
+    panels = one.shape[0]
+
+    def panel(p, acc):
+        value = one[p, pl.ds(at, strip), :]
+        return acc + (value * value).reshape(-1, 8, LANES).sum(axis=0)
+
+    total = lax.fori_loop(0, panels, panel, jnp.zeros((8, LANES), jnp.float32))
+    bands = band_table((8, LANES))
+    row = lax.broadcasted_iota(jnp.int32, (8, LANES), 0)
+    col = lax.broadcasted_iota(jnp.int32, (8, LANES), 1)
+    acc = jnp.zeros((8, LANES), jnp.float32)
+    for s in range(3 * SLEVELS + 1):
+        part = jnp.sum(jnp.where(bands == s, total, 0.0))
+        acc = acc + jnp.where((row == time_band) & (col == s), part, 0.0)
+    return acc
+
+
+def panels_of(ref, width):
+    def own(r, m):
+        return [ref[r:r + m, p * LANES:(p + 1) * LANES] for p in range(width // LANES)]
+    return own
+
+
+def put_strip(one, at, strip, out_plane, sem):
+    return [
+        pltpu.make_async_copy(
+            one.at[p, pl.ds(at, strip)], out_plane.at[:, p * LANES:(p + 1) * LANES], sem.at[p]
+        )
+        for p in range(one.shape[0])
+    ]
+
+
+def time_kernel(
+    foot, blocks_ref, out, halo_out, energy_ref,
+    f, recv, g, o1, o3, s0, h, d2, t0, top, edges, w_ref, one, two, three,
+    in_sem, send_sem, recv_sem, edge_send, edge_recv, out_sem, top_sem, last_sem,
+):
+    strip, width = foot.shape[1:]
+    me, upper = lax.axis_index("frame"), lax.axis_index("row")
+    devices = lax.axis_size("frame")
+    left, right = lax.rem(me + devices - 1, devices), lax.rem(me + 1, devices)
+    first, last = me == 0, me == devices - 1
+    odd = lax.rem(me, 2) == 1
+    size = strip // CHUNKS
+
+    def rows(c):
+        at = jnp.where(upper == 1, c, CHUNKS - 1 - c) * size
+        return pl.ds(pl.multiple_of(at, size), size)
+
+    def send(level, side, c, src, where=None):
+        return pltpu.make_async_remote_copy(
+            src_ref=src.at[rows(c)],
+            dst_ref=recv.at[level, side, rows(c)],
+            send_sem=send_sem.at[level, side, c],
+            recv_sem=recv_sem.at[level, side, c],
+            device_id=(left if side == 0 else right, upper),
+            device_id_type=pl.DeviceIdType.MESH,
+        )
+
+    def send_edge(plane, src):
+        at = pl.multiple_of((strip - HALO) * (1 - upper), HALO)
+        return pltpu.make_async_remote_copy(
+            src_ref=src.at[pl.ds(at, HALO)],
+            dst_ref=edges.at[plane],
+            send_sem=edge_send.at[plane],
+            recv_sem=edge_recv.at[plane],
+            device_id=(me, 1 - upper),
+            device_id_type=pl.DeviceIdType.MESH,
+        )
+
+    def each(body):
+        def step(c, carry):
+            body(c)
+            return carry
+        lax.fori_loop(0, CHUNKS, step, 0)
+
+    loads = [pltpu.make_async_copy(foot.at[n], f.at[n], in_sem.at[n]) for n in range(4)]
+    for n in (3, 2, 0, 1):
+        loads[n].start()
+    barrier = pltpu.get_barrier_semaphore()
+    for where in ((left, upper), (right, upper), (me, 1 - upper)):
+        pl.semaphore_signal(barrier, inc=1, device_id=where, device_id_type=pl.DeviceIdType.MESH)
+    pl.semaphore_wait(barrier, 3)
+
+    each(lambda c: send(0, 0, c, foot.at[0]).start())
+    loads[3].wait()
+    loads[2].wait()
+
+    def first_right(c):
+        r = rows(c)
+        g[r] = f[3, r] - 0.5 * f[2, r]
+        send(0, 1, c, g).start()
+
+    each(first_right)
+    loads[0].wait()
+    loads[1].wait()
+
+    def first_high(c):
+        r = rows(c)
+        o1[r] = f[1, r] - 0.5 * (f[0, r] + f[2, r])
+
+    each(first_high)
+    send_edge(0, o1).start()
+    build_weights(blocks_ref, w_ref)
+    bufs = (one, two, three)
+
+    def plane_out(slot, src, frame, time_band, previous):
+        def before():
+            if previous is not None:
+                for copy in previous:
+                    copy.wait()
+
+        def halo():
+            send_edge(slot, src).wait_recv()
+            return panels_of(edges.at[slot], width)(0, HALO)
+
+        at = spatial(panels_of(src, width), halo, upper, w_ref, bufs, before)
+        copies = put_strip(one, at, strip, out.at[frame], out_sem)
+        for copy in copies:
+            copy.start()
+        return copies, band_energy(one, at, strip, time_band)
+
+    copies, energy1 = plane_out(0, o1, 1, 0, None)
+
+    def second(c):
+        r = rows(c)
+        send(0, 0, c, foot.at[0]).wait_recv()
+        send(0, 1, c, g).wait_recv()
+        f0, f2, first_o = f[0, r], f[2, r], o1[r]
+        o_next = g[r] - 0.5 * jnp.where(last, f2, recv[0, 0, r])
+        o_prev = jnp.where(first, first_o, recv[0, 1, r] - 0.5 * f0)
+        low = f0 + 0.25 * (o_prev + first_o)
+        o3[r] = o_next
+        s0[r] = low
+        h[r] = f2 + 0.25 * (first_o + o_next) - 0.5 * low
+        send(1, 0, c, s0).start()
+        send(1, 1, c, h).start()
+
+        @pl.when(c == 0)
+        def _():
+            send_edge(1, o3).start()
+
+    each(second)
+    copies, energy3 = plane_out(1, o3, 3, 0, copies)
+
+    def third(c):
+        r = rows(c)
+        send(1, 0, c, s0).wait_recv()
+        send(1, 1, c, h).wait_recv()
+        low = s0[r]
+        high = h[r] - 0.5 * jnp.where(last, low, recv[1, 0, r])
+        high_prev = jnp.where(first, high, recv[1, 1, r] - 0.5 * low)
+        d2[r] = high
+        t = low + 0.25 * (high_prev + high)
+
+        @pl.when(jnp.logical_not(odd))
+        def _():
+            t0[r] = t
+            send(2, 1, c, t0).start()
+            send(2, 0, c, t0).start()
+
+        @pl.when(odd)
+        def _():
+            send(2, 1, c, t0).wait_recv()
+            t0[r] = t - 0.5 * recv[2, 1, r]
+            send(2, 1, c, t0).start()
+
+        @pl.when(c == 0)
+        def _():
+            send_edge(2, d2).start()
+
+    each(third)
+    copies, energy2 = plane_out(2, d2, 2, 1, copies)
+
+    def fourth(c):
+        r = rows(c)
+        send(2, 0, c, t0).wait_recv()
+
+        @pl.when(odd)
+        def _():
+            top[r] = t0[r] - 0.5 * jnp.where(last, recv[2, 1, r], recv[2, 0, r])
+            send(2, 0, c, top).start()
+
+        @pl.when(jnp.logical_not(odd))
+        def _():
+            send(2, 1, c, t0).wait_recv()
+            mine, after = t0[r], recv[2, 0, r]
+            prev = jnp.where(first, after, recv[2, 1, r] - 0.5 * mine)
+            top[r] = mine + 0.25 * (prev + after)
+
+        pltpu.make_async_copy(top.at[r], out.at[0, r], top_sem.at[c]).start()
+
+        @pl.when(c == 0)
+        def _():
+            send_edge(3, top).start()
+
+    each(fourth)
+    energy_ref[...] = energy1 + energy2 + energy3
+    send_edge(3, top).wait_recv()
+    tail = pltpu.make_async_copy(edges.at[3], halo_out, last_sem)
+    tail.start()
+    for copy in copies:
+        copy.wait()
+    for plane, src in enumerate((o1, o3, d2, top)):
+        send_edge(plane, src).wait_send()
+
+    def drain(c):
+        send(0, 0, c, foot.at[0]).wait_send()
+        send(0, 1, c, g).wait_send()
+        send(1, 0, c, s0).wait_send()
+        send(1, 1, c, h).wait_send()
+        send(2, 0, c, top).wait_send()
+        send(2, 1, c, t0).wait_send()
+        pltpu.make_async_copy(top.at[rows(c)], out.at[0, rows(c)], top_sem.at[c]).wait()
+
+    each(drain)
+    tail.wait()
+
+
+def finish_kernel(planes, halo_ref, blocks_ref, part_ref, out, energy_ref, mine, stage, w_ref, one, two, three, in_sem, stage_sem, out_sem):
+    strip, width = planes.shape[1:]
+    upper = lax.axis_index("row")
+    odd = lax.rem(lax.axis_index("frame"), 2) == 1
+    load = pltpu.make_async_copy(planes.at[0], mine, in_sem)
+    load.start()
+    takes = [pltpu.make_async_copy(planes.at[n + 1], stage.at[n], stage_sem.at[0, n]) for n in range(3)]
+    puts = [pltpu.make_async_copy(stage.at[n], out.at[n + 1], stage_sem.at[1, n]) for n in range(3)]
+    for take in takes:
+        take.start()
+    build_weights(blocks_ref, w_ref)
+    load.wait()
+
+    def midway():
+        for take, put in zip(takes, puts):
+            take.wait()
+            put.start()
+
+    halo = lambda: panels_of(halo_ref, width)(0, HALO)
+    at = spatial(panels_of(mine, width), halo, upper, w_ref, (one, two, three), midway=midway)
+    copies = put_strip(one, at, strip, out.at[0], out_sem)
+    for copy in copies:
+        copy.start()
+    energy_ref[...] = part_ref[...] + band_energy(one, at, strip, jnp.where(odd, 2, 3))
+    for copy in copies + puts:
+        copy.wait()
+
+
+def spatial_scratch(strip, width):
+    panels, rows = width // LANES, strip + HALO
+    return [pltpu.VMEM((SLEVELS, 2, 3, 4 * LANES, 2 * LANES), jnp.bfloat16)] + [
+        pltpu.VMEM((panels, rows // k + 2 * PAD, LANES), jnp.float32) for k in (1, 2, 4)
+    ]
+
+
 def shards(footage):
-    me = lax.axis_index("frame")
+    frames, strip, width = footage.shape
+    blocks = jnp.asarray(weight_blocks(width))
+    plane = pltpu.VMEM((strip, width), jnp.float32)
+    dma = pltpu.SemaphoreType.DMA
+    full = jax.ShapeDtypeStruct(footage.shape, jnp.float32)
+    tile = jax.ShapeDtypeStruct((8, LANES), jnp.float32)
+    hbm = pl.BlockSpec(memory_space=pl.ANY)
+    vmem = pl.BlockSpec(memory_space=pltpu.VMEM)
+    planes, edge, part = pl.pallas_call(
+        time_kernel,
+        out_shape=(full, jax.ShapeDtypeStruct((HALO, width), jnp.float32), tile),
+        in_specs=[hbm, vmem],
+        out_specs=(hbm, hbm, vmem),
+        scratch_shapes=[
+            pltpu.VMEM(footage.shape, jnp.float32),
+            pltpu.VMEM((3, 2, strip, width), jnp.float32),
+            *[plane] * 8,
+            pltpu.VMEM((4, HALO, width), jnp.float32),
+            *spatial_scratch(strip, width),
+            dma((4,)),
+            dma((3, 2, CHUNKS)),
+            dma((3, 2, CHUNKS)),
+            dma((4,)),
+            dma((4,)),
+            dma((width // LANES,)),
+            dma((CHUNKS,)),
+            dma,
+        ],
+        compiler_params=pltpu.CompilerParams(
+            collective_id=0, has_side_effects=True, vmem_limit_bytes=60 * 2**20
+        ),
+        name="time",
+    )(footage, blocks)
+    coeffs, energy = pl.pallas_call(
+        finish_kernel,
+        out_shape=(full, tile),
+        in_specs=[hbm, vmem, vmem, vmem],
+        out_specs=(hbm, vmem),
+        scratch_shapes=[
+            plane,
+            pltpu.VMEM((3, strip, width), jnp.float32),
+            *spatial_scratch(strip, width),
+            dma,
+            dma((2, 3)),
+            dma((width // LANES,)),
+        ],
+        compiler_params=pltpu.CompilerParams(vmem_limit_bytes=40 * 2**20),
+        name="finish",
+    )(planes, edge, blocks, part)
+    total = lax.psum(energy, ("frame", "row"))[:TLEVELS + 1, :3 * SLEVELS + 1]
     devices = lax.axis_size("frame")
-    first, last = me == 0, me == devices - 1
-    odd = me % 2 == 1
-    left = lambda x: lax.ppermute(x, "frame", [(i, i - 1) for i in range(1, devices)])
-    right = lambda x: lax.ppermute(x, "frame", [(i, i + 1) for i in range(devices - 1)])
-    f0, f1, f2, f3 = footage[0], footage[1], footage[2], footage[3]
-    g = f3 - 0.5 * f2
-    f4 = left(f0)
-    g_prev = right(g)
-    o1 = f1 - 0.5 * (f0 + f2)
-    o3 = g - 0.5 * jnp.where(last, f2, f4)
-    o_prev = jnp.where(first, o1, g_prev - 0.5 * f0)
-    s0 = f0 + 0.25 * (o_prev + o1)
-    s2 = f2 + 0.25 * (o1 + o3)
-    h = s2 - 0.5 * s0
-    s4 = left(s0)
-    h_prev = right(h)
-    d2 = h - 0.5 * jnp.where(last, s0, s4)
-    d_prev = jnp.where(first, d2, h_prev - 0.5 * s0)
-    t0 = s0 + 0.25 * (d_prev + d2)
-    t_next = left(t0)
-    t_prev = right(t0)
-    p = t0 - 0.5 * t_prev
-    high = p - 0.5 * jnp.where(last, t_prev, t_next)
-    sent = jnp.where(odd, high, 0.0)
-    hi_next = left(sent)
-    hi_prev = right(sent)
-    low = t0 + 0.25 * (jnp.where(first, hi_next, hi_prev) + hi_next)
-    top = jnp.where(odd, high, low)
-    coeffs = jnp.stack([top, o1, d2, o3])
-    upper = lax.axis_index("row")
-    strip = coeffs.shape[1]
-    edge = jnp.where(upper == 0, coeffs[:, strip - HALO:], coeffs[:, :HALO])
-    halos = lax.ppermute(edge, "row", [(0, 1), (1, 0)])
-    out, energy = spatial_call(coeffs, halos)
-    total = lax.psum(energy, ("frame", "row"))[:4, :3 * SLEVELS + 1]
-    size = counts(4 * devices, strip * lax.axis_size("row"), footage.shape[2])
-    return out, total / jnp.asarray(size, jnp.float32)
+    size = counts(frames * devices, strip * lax.axis_size("row"), width)
+    return coeffs, total / jnp.asarray(size, jnp.float32)
 
 
 def solution(mesh):

time: 290 us -> 216 us (0.74)
  waiting for transfers between devices: 123 us -> 0 us
  Pallas kernels: 28.4 us -> 133 us
  other arithmetic: 35.9 us -> 0.58 us
  starting transfers between devices: 26.9 us -> 0 us
  local copies, waits for them, and re-layouts: 0.03 us -> 4.96 us
    ppermute x9 -> x0, waiting for transfers between devices: 123 us -> none  [the longest x4 60.4 us: shards(): lax.ppermute(x, 'frame', [(i, i + 1) for i in range(devices - 1)])]
    pallas_call x1 -> x2, Pallas kernels: 28.4 us -> 133 us  [the longest x1 124 us: shards(): pl.pallas_call(time_kernel, out_shape=(full, jax.ShapeDtypeStruct((HALO,...]
    ppermute x9 -> x0, starting transfers between devices: 26.9 us -> none  [the longest x4 15.4 us: shards(): lax.ppermute(x, 'frame', [(i, i + 1) for i in range(devices - 1)])]
    another operation x3 -> x0, other arithmetic: 14.6 us -> none  [shards(): coeffs = jnp.stack([top, o1, d2, o3])]
    sub x2 -> x0, other arithmetic: 8.65 us -> none  [the longest x1 6 us: shards(): o1 = f1 - 0.5 * (f0 + f2)]
    add x2 -> x0, other arithmetic: 7.71 us -> none  [the longest x1 4.48 us: shards(): s0 = f0 + 0.25 * (o_prev + o1)]
    unnamed x12 -> x10, local copies, waits for them, and re-layouts: 0.03 us -> 4.96 us
    select_n x2 -> x0, other arithmetic: 4.36 us -> none  [the longest x1 4.29 us: shards(): sent = jnp.where(odd, high, 0.0)]
  transfers between devices with their start and end apart: 9 -> 0, of which waited for: 9 -> 0; matrix products, arithmetic and copies ran while one was open for 4% -> 0% of each run, Pallas kernels for 0% -> 0%
where the time goes in v2:
time: 216 us
  Pallas kernels  133 us (62%)
  blocking collectives  76.6 us (35%)
  local copies, waits for them, and re-layouts  4.96 us (2%)
    pallas_call x1, Pallas kernels, shards(): pl.pallas_call(time_kernel, out_shape=(full, jax.ShapeDtypeStruct((HALO,...  124 us
    psum x1, blocking collectives, shards(): total = lax.psum(energy, ('frame', 'row'))[:TLEVELS + 1, :3 * SLEVELS + 1]  76.6 us
    pallas_call x1, Pallas kernels, shards(): pl.pallas_call(finish_kernel, out_shape=(full, tile), in_specs=[hbm, vmem...  8.99 us
    unnamed x10, local copies, waits for them, and re-layouts  4.96 us

profile of v2, /device:TPU:1, one launch (start us, length us, event | category | flops | bytes accessed | tf_op | source)
XLA Modules:
  0.0 215.7 jit_solution(4501538462242461663)
XLA Ops:
  0.6 0.0 copy-start.1
  0.6 0.0 copy-start.4
  0.7 123.9 %time.1 = (f32[4,512,1024]{2,1,0:T(8,128)}, f32[32,1024]{1,0:T(8,128)}, f32[8,128]{1,0:T(8,128)}) custom-call(f32[4,512,1024]{2,1,0:T(8,128)} %foot.1, bf16[3,2,5,128,128]{4,3,2,1,0:T(8,128)(2,1)} %constant.4.clone.blocks_ref), custom_call_target="tpu_custom_call" | custom-call | tf_op jit(solution)/shard_map/time/pallas_call | solution.py:491
  124.6 0.0 copy-done.1
  124.6 0.0 copy-start
  124.6 3.4 %copy-done = f32[4,512,1024]{2,1,0:T(8,128)S(1)} copy-done((f32[4,512,1024]{2,1,0:T(8,128)S(1)}, f32[4,512,1024]{2,1,0:T(8,128)}, u32[]{:S(2)}) %copy-start) | copy-done | bytes 8388632
  127.9 0.0 copy-start.2
  127.9 0.9 copy-done.2
  128.8 0.0 copy-start.3
  128.9 0.7 copy-done.3
  129.5 9.0 %finish.1 = (f32[4,512,1024]{2,1,0:T(8,128)}, f32[8,128]{1,0:T(8,128)S(1)}) custom-call(f32[4,512,1024]{2,1,0:T(8,128)S(1)} %copy-done, f32[32,1024]{1,0:T(8,128)S(1)} %copy-done.2, bf16[3,2,5,128,128]{4,3,2,1,0:T(8,128)(2,1)S(1)} %copy-done.1, f32[8,128]{1,0:T(8,128)S(1)} %copy-done.3), custom_call_target="tpu_custom_call" | custom-call | tf_op jit(solution)/shard_map/finish/pallas_call | solution.py:516
  138.5 76.6 %psum.7 = f32[8,128]{1,0:T(8,128)S(1)} all-reduce(f32[8,128]{1,0:T(8,128)S(1)} %get-tuple-element.11), channel_id=1, replica_groups=mesh['frame'=64,'row'=2] {'frame','row'}, use_global_device_ids=true, to_apply=%region_0.0 | all-reduce | flops 1024 | bytes 8192 | tf_op jit(solution)/shard_map/psum | solution.py:532
  215.1 0.0 copy-done.4
  215.1 0.6 slice_multiply_fusion
Async XLA Ops:
  0.6 123.9 %copy-start.1 = (bf16[3,2,5,128,128]{4,3,2,1,0:T(8,128)(2,1)S(1)}, bf16[3,2,5,128,128]{4,3,2,1,0:T(8,128)(2,1)}, u32[]{:S(2)}) copy-start(bf16[3,2,5,128,128]{4,3,2,1,0:T(8,128)(2,1)} %constant.4.clone.blocks_ref) | copy-start | bytes 2949124
  0.6 214.5 %copy-start.4 = (f32[4,10]{1,0:T(4,128)S(1)}, f32[4,10]{1,0:T(4,128)}, u32[]{:S(2)}) copy-start(f32[4,10]{1,0:T(4,128)} %constant.7) | copy-start | bytes 484
  124.6 3.4 %copy-start = (f32[4,512,1024]{2,1,0:T(8,128)S(1)}, f32[4,512,1024]{2,1,0:T(8,128)}, u32[]{:S(2)}) copy-start(f32[4,512,1024]{2,1,0:T(8,128)} %get-tuple-element.7.planes) | copy-start | bytes 25165828
  127.9 0.9 copy-start.2
  128.8 0.7 copy-start.3

commit v3 on v2

--- a/solution.py
+++ b/solution.py
@@ -20,6 +20,7 @@
 PAD = 8
 LANES = 128
 CHUNKS = 8
+Y_CHIPS = 4
 
 
 def lift_matrix(width):
@@ -132,30 +133,33 @@
     lax.fori_loop(0, buf.shape[0], panel, 0)
 
 
-def spatial(own, halo, upper, w_ref, bufs, before=None, midway=None):
+def strip_rows(one, upper):
+    strip = one.shape[1] - 2 * PAD - HALO
+    own_at = pl.multiple_of(PAD + HALO * upper, 8)
+    halo_at = pl.multiple_of(PAD + strip * (1 - upper), 8)
+    return strip, own_at, halo_at
+
+
+def first_columns(own, halo, upper, w_ref, one):
+    strip, own_at, halo_at = strip_rows(one, upper)
+    half = strip // 2
+
+    def store_top(p, value):
+        one[p, pl.ds(own_at, half), :] = value
+
+    def store_rest(p, value):
+        one[p, pl.ds(pl.multiple_of(own_at + half, 8), half), :] = value[:half]
+        one[p, pl.ds(halo_at, HALO), :] = value[half:]
+
+    columns(own(0, half), w_ref, 0, store_top)
+    rest = [jnp.concatenate(pair, axis=0) for pair in zip(own(half, half), halo())]
+    columns(rest, w_ref, 0, store_rest)
+
+
+def after_first_columns(w_ref, bufs):
     one, two, three = bufs
     panels = one.shape[0]
     rows = one.shape[1] - 2 * PAD
-    strip = rows - HALO
-    half = strip // 2
-    own_at = pl.multiple_of(PAD + HALO * upper, 8)
-    rest_at = pl.multiple_of(PAD + HALO * upper + half, 8)
-    halo_at = pl.multiple_of(PAD + strip * (1 - upper), 8)
-
-    def store_top(p, value):
-        one[p, pl.ds(own_at, half), :] = value
-
-    def store_rest(p, value):
-        one[p, pl.ds(rest_at, half), :] = value[:half]
-        one[p, pl.ds(halo_at, HALO), :] = value[half:]
-
-    if before is not None:
-        before()
-    columns(own(0, half), w_ref, 0, store_top)
-    rest = [jnp.concatenate(pair, axis=0) for pair in zip(own(half, half), halo())]
-    columns(rest, w_ref, 0, store_rest)
-    if midway is not None:
-        midway()
     lift_rows(one, rows // 2)
 
     def into(buf, n):
@@ -182,7 +186,6 @@
         return carry
 
     lax.fori_loop(0, panels, merge, 0)
-    return own_at
 
 
 def level_of(number, ceiling):
@@ -258,9 +261,9 @@
 
 
 def time_kernel(
-    foot, blocks_ref, out, halo_out, energy_ref,
-    f, recv, g, o1, o3, s0, h, d2, t0, top, edges, w_ref, one, two, three,
-    in_sem, send_sem, recv_sem, edge_send, edge_recv, out_sem, top_sem, last_sem,
+    foot, blocks_ref, counts_ref, out, energy_ref,
+    f, recv, g, o1, o3, s0, h, d2, t0, top, edges, shared, w_ref, one, two, three,
+    in_sem, send_sem, recv_sem, edge_send, edge_recv, out_sem, sum_send, sum_recv,
 ):
     strip, width = foot.shape[1:]
     me, upper = lax.axis_index("frame"), lax.axis_index("row")
@@ -295,19 +298,35 @@
             device_id_type=pl.DeviceIdType.MESH,
         )
 
-    def each(body):
+    def each(body, begin=0, end=CHUNKS):
         def step(c, carry):
             body(c)
             return carry
-        lax.fori_loop(0, CHUNKS, step, 0)
+        lax.fori_loop(begin, end, step, 0)
+
+    ring = 2 * Y_CHIPS
+    x_at, z_at, y_at = me // (2 * ring), lax.rem(me // ring, 2), lax.rem(me, ring)
+    base = me - y_at
+    groups = (
+        (y_at, [(base + k, upper) for k in range(ring)]),
+        (x_at, [(me + (k - x_at) * 2 * ring, upper) for k in range(devices // (2 * ring))]),
+        (z_at + 2 * upper, [(me + (k % 2 - z_at) * ring, k // 2) for k in range(4)]),
+    )
 
     loads = [pltpu.make_async_copy(foot.at[n], f.at[n], in_sem.at[n]) for n in range(4)]
     for n in (3, 2, 0, 1):
         loads[n].start()
     barrier = pltpu.get_barrier_semaphore()
-    for where in ((left, upper), (right, upper), (me, 1 - upper)):
+
+    def greet(where):
         pl.semaphore_signal(barrier, inc=1, device_id=where, device_id_type=pl.DeviceIdType.MESH)
-    pl.semaphore_wait(barrier, 3)
+
+    for where in ((left, upper), (right, upper)):
+        greet(where)
+    for slot, members in groups:
+        for k, where in enumerate(members):
+            pl.when(slot != k)(functools.partial(greet, where))
+    pl.semaphore_wait(barrier, 2 + sum(len(members) - 1 for _, members in groups))
 
     each(lambda c: send(0, 0, c, foot.at[0]).start())
     loads[3].wait()
@@ -326,28 +345,30 @@
         r = rows(c)
         o1[r] = f[1, r] - 0.5 * (f[0, r] + f[2, r])
 
-    each(first_high)
+    first_high(0)
     send_edge(0, o1).start()
+    each(first_high, 1)
     build_weights(blocks_ref, w_ref)
     bufs = (one, two, three)
 
     def plane_out(slot, src, frame, time_band, previous):
-        def before():
-            if previous is not None:
-                for copy in previous:
-                    copy.wait()
+        for copy in previous:
+            copy.wait()
 
         def halo():
             send_edge(slot, src).wait_recv()
             return panels_of(edges.at[slot], width)(0, HALO)
 
-        at = spatial(panels_of(src, width), halo, upper, w_ref, bufs, before)
-        copies = put_strip(one, at, strip, out.at[frame], out_sem)
+        first_columns(panels_of(src, width), halo, upper, w_ref, one)
+        return rest_out(frame, time_band)
+
+    def rest_out(frame, time_band):
+        after_first_columns(w_ref, bufs)
+        own_at = strip_rows(one, upper)[1]
+        copies = put_strip(one, own_at, strip, out.at[frame], out_sem)
         for copy in copies:
             copy.start()
-        return copies, band_energy(one, at, strip, time_band)
-
-    copies, energy1 = plane_out(0, o1, 1, 0, None)
+        return copies, band_energy(one, own_at, strip, time_band)
 
     def second(c):
         r = rows(c)
@@ -367,7 +388,9 @@
         def _():
             send_edge(1, o3).start()
 
-    each(second)
+    each(second, 0, CHUNKS // 2)
+    copies, energy1 = plane_out(0, o1, 1, 0, [])
+    each(second, CHUNKS // 2)
     copies, energy3 = plane_out(1, o3, 3, 0, copies)
 
     def third(c):
@@ -398,6 +421,9 @@
 
     each(third)
     copies, energy2 = plane_out(2, d2, 2, 1, copies)
+    for copy in copies:
+        copy.wait()
+    own_at, halo_at = strip_rows(one, upper)[1:]
 
     def fourth(c):
         r = rows(c)
@@ -415,17 +441,61 @@
             prev = jnp.where(first, after, recv[2, 1, r] - 0.5 * mine)
             top[r] = mine + 0.25 * (prev + after)
 
-        pltpu.make_async_copy(top.at[r], out.at[0, r], top_sem.at[c]).start()
-
         @pl.when(c == 0)
         def _():
             send_edge(3, top).start()
 
+        def store(p, value):
+            one[p, pl.ds(pl.multiple_of(own_at + r.start, 8), size), :] = value
+
+        columns([top[r, p * LANES:(p + 1) * LANES] for p in range(width // LANES)], w_ref, 0, store)
+
+        @pl.when(c == CHUNKS - 2)
+        def _():
+            send_edge(3, top).wait_recv()
+
+            def store_halo(p, value):
+                one[p, pl.ds(halo_at, HALO), :] = value
+
+            columns(panels_of(edges.at[3], width)(0, HALO), w_ref, 0, store_halo)
+
     each(fourth)
-    energy_ref[...] = energy1 + energy2 + energy3
-    send_edge(3, top).wait_recv()
-    tail = pltpu.make_async_copy(edges.at[3], halo_out, last_sem)
-    tail.start()
+    copies, energy0 = rest_out(0, jnp.where(odd, 2, 3))
+    total = energy0 + energy1 + energy2 + energy3
+
+    def tell(stage, k):
+        slot, members = groups[stage]
+        return pltpu.make_async_remote_copy(
+            src_ref=shared.at[stage, slot],
+            dst_ref=shared.at[stage, slot],
+            send_sem=sum_send.at[stage, k],
+            recv_sem=sum_recv.at[stage, slot],
+            device_id=members[k],
+            device_id_type=pl.DeviceIdType.MESH,
+        )
+
+    def heard(stage, k):
+        return pltpu.make_async_remote_copy(
+            src_ref=shared.at[stage, k],
+            dst_ref=shared.at[stage, k],
+            send_sem=sum_send.at[stage, k],
+            recv_sem=sum_recv.at[stage, k],
+            device_id=groups[stage][1][k],
+            device_id_type=pl.DeviceIdType.MESH,
+        )
+
+    for stage, (slot, members) in enumerate(groups):
+        shared[stage, slot] = total
+        for k in range(len(members)):
+            pl.when(slot != k)(lambda stage=stage, k=k: tell(stage, k).start())
+        for k in range(len(members)):
+            pl.when(slot != k)(lambda stage=stage, k=k: heard(stage, k).wait_recv())
+        total = functools.reduce(jnp.add, [shared[stage, k] for k in range(len(members))])
+    energy_ref[...] = total[:TLEVELS + 1, :3 * SLEVELS + 1] / counts_ref[...]
+
+    for stage, (slot, members) in enumerate(groups):
+        for k in range(len(members)):
+            pl.when(slot != k)(lambda stage=stage, k=k: tell(stage, k).wait_send())
     for copy in copies:
         copy.wait()
     for plane, src in enumerate((o1, o3, d2, top)):
@@ -438,38 +508,8 @@
         send(1, 1, c, h).wait_send()
         send(2, 0, c, top).wait_send()
         send(2, 1, c, t0).wait_send()
-        pltpu.make_async_copy(top.at[rows(c)], out.at[0, rows(c)], top_sem.at[c]).wait()
 
     each(drain)
-    tail.wait()
-
-
-def finish_kernel(planes, halo_ref, blocks_ref, part_ref, out, energy_ref, mine, stage, w_ref, one, two, three, in_sem, stage_sem, out_sem):
-    strip, width = planes.shape[1:]
-    upper = lax.axis_index("row")
-    odd = lax.rem(lax.axis_index("frame"), 2) == 1
-    load = pltpu.make_async_copy(planes.at[0], mine, in_sem)
-    load.start()
-    takes = [pltpu.make_async_copy(planes.at[n + 1], stage.at[n], stage_sem.at[0, n]) for n in range(3)]
-    puts = [pltpu.make_async_copy(stage.at[n], out.at[n + 1], stage_sem.at[1, n]) for n in range(3)]
-    for take in takes:
-        take.start()
-    build_weights(blocks_ref, w_ref)
-    load.wait()
-
-    def midway():
-        for take, put in zip(takes, puts):
-            take.wait()
-            put.start()
-
-    halo = lambda: panels_of(halo_ref, width)(0, HALO)
-    at = spatial(panels_of(mine, width), halo, upper, w_ref, (one, two, three), midway=midway)
-    copies = put_strip(one, at, strip, out.at[0], out_sem)
-    for copy in copies:
-        copy.start()
-    energy_ref[...] = part_ref[...] + band_energy(one, at, strip, jnp.where(odd, 2, 3))
-    for copy in copies + puts:
-        copy.wait()
 
 
 def spatial_scratch(strip, width):
@@ -485,19 +525,21 @@
     plane = pltpu.VMEM((strip, width), jnp.float32)
     dma = pltpu.SemaphoreType.DMA
     full = jax.ShapeDtypeStruct(footage.shape, jnp.float32)
-    tile = jax.ShapeDtypeStruct((8, LANES), jnp.float32)
     hbm = pl.BlockSpec(memory_space=pl.ANY)
     vmem = pl.BlockSpec(memory_space=pltpu.VMEM)
-    planes, edge, part = pl.pallas_call(
+    devices = lax.axis_size("frame")
+    size = counts(frames * devices, strip * lax.axis_size("row"), width)
+    return pl.pallas_call(
         time_kernel,
-        out_shape=(full, jax.ShapeDtypeStruct((HALO, width), jnp.float32), tile),
-        in_specs=[hbm, vmem],
-        out_specs=(hbm, hbm, vmem),
+        out_shape=(full, jax.ShapeDtypeStruct(size.shape, jnp.float32)),
+        in_specs=[hbm, vmem, vmem],
+        out_specs=(hbm, vmem),
         scratch_shapes=[
             pltpu.VMEM(footage.shape, jnp.float32),
             pltpu.VMEM((3, 2, strip, width), jnp.float32),
             *[plane] * 8,
             pltpu.VMEM((4, HALO, width), jnp.float32),
+            pltpu.VMEM((3, 2 * Y_CHIPS, 8, LANES), jnp.float32),
             *spatial_scratch(strip, width),
             dma((4,)),
             dma((3, 2, CHUNKS)),
@@ -505,34 +547,14 @@
             dma((4,)),
             dma((4,)),
             dma((width // LANES,)),
-            dma((CHUNKS,)),
-            dma,
+            dma((3, 2 * Y_CHIPS)),
+            dma((3, 2 * Y_CHIPS)),
         ],
         compiler_params=pltpu.CompilerParams(
             collective_id=0, has_side_effects=True, vmem_limit_bytes=60 * 2**20
         ),
         name="time",
-    )(footage, blocks)
-    coeffs, energy = pl.pallas_call(
-        finish_kernel,
-        out_shape=(full, tile),
-        in_specs=[hbm, vmem, vmem, vmem],
-        out_specs=(hbm, vmem),
-        scratch_shapes=[
-            plane,
-            pltpu.VMEM((3, strip, width), jnp.float32),
-            *spatial_scratch(strip, width),
-            dma,
-            dma((2, 3)),
-            dma((width // LANES,)),
-        ],
-        compiler_params=pltpu.CompilerParams(vmem_limit_bytes=40 * 2**20),
-        name="finish",
-    )(planes, edge, blocks, part)
-    total = lax.psum(energy, ("frame", "row"))[:TLEVELS + 1, :3 * SLEVELS + 1]
-    devices = lax.axis_size("frame")
-    size = counts(frames * devices, strip * lax.axis_size("row"), width)
-    return coeffs, total / jnp.asarray(size, jnp.float32)
+    )(footage, blocks, jnp.asarray(size, jnp.float32))
 
 
 def solution(mesh):

time: 216 us -> 143 us (0.66)
  blocking collectives: 76.6 us -> 0 us
  local copies, waits for them, and re-layouts: 4.96 us -> 9.02 us
    psum x1 -> x0, blocking collectives: 76.6 us -> none  [shards(): total = lax.psum(energy, ('frame', 'row'))[:TLEVELS + 1, :3 * SLEVELS + 1]]
    unnamed x10 -> x4, local copies, waits for them, and re-layouts: 4.96 us -> 9.02 us
    pallas_call x2 -> x1, Pallas kernels: 133 us -> 131 us  [shards(): pl.pallas_call(time_kernel, out_shape=(full, jax.ShapeDtypeStruct(size.sh...]
where the time goes in v3:
time: 143 us; the launch traced here: 141 us
  Pallas kernels  131 us (92%)
  local copies, waits for them, and re-layouts  9.02 us (6%)
    pallas_call x1, Pallas kernels, shards(): pl.pallas_call(time_kernel, out_shape=(full, jax.ShapeDtypeStruct(size.sh...  131 us
    unnamed x4, local copies, waits for them, and re-layouts  9.02 us

profile of v3, /device:TPU:1, one launch (start us, length us, event | category | flops | bytes accessed | tf_op | source)
XLA Modules:
  0.0 140.9 jit_solution(13319095399999533278)
XLA Ops:
  0.6 131.3 %time.1 = (f32[4,512,1024]{2,1,0:T(8,128)}, f32[4,10]{1,0:T(4,128)}) custom-call(f32[4,512,1024]{2,1,0:T(8,128)} %foot.1, bf16[3,2,5,128,128]{4,3,2,1,0:T(8,128)(2,1)} %constant.4.clone.blocks_ref, f32[4,10]{1,0:T(4,128)} %constant.5.clone.counts_ref), custom_call_target="tpu_custom_call" | custom-call | tf_op jit(solution)/shard_map/time/pallas_call | solution.py:532
  131.9 0.0 copy-start
  131.9 8.4 %copy.7 = f32[4,512,1024]{2,1,0:T(8,128)} copy(f32[4,512,1024]{2,1,0:T(8,128)} %get-tuple-element.4) | data formatting | bytes 16777216
  140.3 0.0 copy-done
  140.4 0.6 copy.8
Async XLA Ops:
  131.9 8.5 %copy-start = (f32[4,10]{1,0:T(4,128)S(1)}, f32[4,10]{1,0:T(4,128)}, u32[]{:S(2)}) copy-start(f32[4,10]{1,0:T(4,128)} %get-tuple-element.5) | copy-start | bytes 484

commit v4 on v3

--- a/solution.py
+++ b/solution.py
@@ -20,6 +20,8 @@
 PAD = 8
 LANES = 128
 CHUNKS = 8
+RANK = 2 * SLEVELS
+EXTRA = 8
 Y_CHIPS = 4
 
 
@@ -64,6 +66,24 @@
     ((3, None), (1, 3), (4, 1), (None, 4)),
     ((None, None), (3, None), (1, 3), (4, 2)),
 )
+
+
+def summaries():
+    n = 4 * HALO
+    steps, done = [], np.eye(n)
+    for level in range(SLEVELS):
+        s = 2**level
+        step = np.eye(n)
+        step[::s, ::s] = lift_matrix(n // s).T
+        done = step @ done
+        steps.append(done)
+    half = n // 2
+    result = np.zeros((2, HALO, LANES))
+    for side, (mine, other) in enumerate(((slice(half, n), slice(half - HALO, half)), (slice(0, half), slice(half, half + HALO)))):
+        cross = np.concatenate([m[mine, other] for m in steps])
+        basis = np.linalg.svd(cross)[2][:RANK]
+        result[side, :, :RANK] = basis.T
+    return result.astype(np.float32)
 
 
 def build_weights(blocks_ref, w_ref):
@@ -261,9 +281,9 @@
 
 
 def time_kernel(
-    foot, blocks_ref, counts_ref, out, energy_ref,
-    f, recv, g, o1, o3, s0, h, d2, t0, top, edges, shared, w_ref, one, two, three,
-    in_sem, send_sem, recv_sem, edge_send, edge_recv, out_sem, sum_send, sum_recv,
+    foot, blocks_ref, basis_ref, counts_ref, out, energy_ref,
+    f, recv, g, o1, o3, s0, h, d2, t0, top, border, summary, shared, w_ref, one, two, three,
+    in_sem, border_sem, send_sem, recv_sem, across, out_sem, sum_send, sum_recv,
 ):
     strip, width = foot.shape[1:]
     me, upper = lax.axis_index("frame"), lax.axis_index("row")
@@ -274,10 +294,11 @@
     size = strip // CHUNKS
 
     def rows(c):
-        at = jnp.where(upper == 1, c, CHUNKS - 1 - c) * size
-        return pl.ds(pl.multiple_of(at, size), size)
-
-    def send(level, side, c, src, where=None):
+        if isinstance(c, int) and c == CHUNKS:
+            return pl.ds(strip, EXTRA)
+        return pl.ds(pl.multiple_of(c * size, size), size)
+
+    def send(level, side, c, src):
         return pltpu.make_async_remote_copy(
             src_ref=src.at[rows(c)],
             dst_ref=recv.at[level, side, rows(c)],
@@ -287,17 +308,6 @@
             device_id_type=pl.DeviceIdType.MESH,
         )
 
-    def send_edge(plane, src):
-        at = pl.multiple_of((strip - HALO) * (1 - upper), HALO)
-        return pltpu.make_async_remote_copy(
-            src_ref=src.at[pl.ds(at, HALO)],
-            dst_ref=edges.at[plane],
-            send_sem=edge_send.at[plane],
-            recv_sem=edge_recv.at[plane],
-            device_id=(me, 1 - upper),
-            device_id_type=pl.DeviceIdType.MESH,
-        )
-
     def each(body, begin=0, end=CHUNKS):
         def step(c, carry):
             body(c)
@@ -313,7 +323,10 @@
         (z_at + 2 * upper, [(me + (k % 2 - z_at) * ring, k // 2) for k in range(4)]),
     )
 
-    loads = [pltpu.make_async_copy(foot.at[n], f.at[n], in_sem.at[n]) for n in range(4)]
+    border_at = pl.multiple_of((strip - HALO) * (1 - upper), HALO)
+    borders = pltpu.make_async_copy(foot.at[:, pl.ds(border_at, HALO)], border, border_sem)
+    borders.start()
+    loads = [pltpu.make_async_copy(foot.at[n], f.at[n, pl.ds(0, strip)], in_sem.at[n]) for n in range(4)]
     for n in (3, 2, 0, 1):
         loads[n].start()
     barrier = pltpu.get_barrier_semaphore()
@@ -326,40 +339,67 @@
     for slot, members in groups:
         for k, where in enumerate(members):
             pl.when(slot != k)(functools.partial(greet, where))
+
+    borders.wait()
+    for n in range(4):
+        values = border[n]
+        for k in range(RANK):
+            summary[n, k:k + 1, :] = (basis_ref[upper, :, k:k + 1] * values).sum(axis=0, keepdims=True)
+        summary[n, RANK:, :] = jnp.zeros((EXTRA - RANK, width), jnp.float32)
+    exchange = pltpu.make_async_remote_copy(
+        src_ref=summary,
+        dst_ref=f.at[:, pl.ds(strip, EXTRA)],
+        send_sem=across.at[0],
+        recv_sem=across.at[1],
+        device_id=(me, 1 - upper),
+        device_id_type=pl.DeviceIdType.MESH,
+    )
     pl.semaphore_wait(barrier, 2 + sum(len(members) - 1 for _, members in groups))
-
-    each(lambda c: send(0, 0, c, foot.at[0]).start())
-    loads[3].wait()
-    loads[2].wait()
-
-    def first_right(c):
+    exchange.start()
+
+    def first_left():
+        each(lambda c: send(0, 0, c, foot.at[0]).start())
+
+    def first_right():
+        each(lambda c: send(0, 1, c, g).start())
+
+    def partial(c):
         r = rows(c)
         g[r] = f[3, r] - 0.5 * f[2, r]
-        send(0, 1, c, g).start()
-
-    each(first_right)
-    loads[0].wait()
-    loads[1].wait()
 
     def first_high(c):
         r = rows(c)
         o1[r] = f[1, r] - 0.5 * (f[0, r] + f[2, r])
 
-    first_high(0)
-    send_edge(0, o1).start()
-    each(first_high, 1)
+    pl.when(y_at != 0)(first_left)
+    loads[3].wait()
+    loads[2].wait()
+    each(partial)
+    pl.when(y_at != ring - 1)(first_right)
+    loads[0].wait()
+    loads[1].wait()
+    each(first_high)
+    exchange.wait_recv()
+    pl.when(y_at == 0)(first_left)
+    pl.when(y_at == ring - 1)(first_right)
+    partial(CHUNKS)
+    first_high(CHUNKS)
+    send(0, 0, CHUNKS, f.at[0]).start()
+    send(0, 1, CHUNKS, g).start()
     build_weights(blocks_ref, w_ref)
     bufs = (one, two, three)
 
-    def plane_out(slot, src, frame, time_band, previous):
+    def halo_of(src):
+        values = src[rows(CHUNKS)]
+        total = basis_ref[1 - upper, :, 0:1] * values[0:1]
+        for k in range(1, RANK):
+            total = total + basis_ref[1 - upper, :, k:k + 1] * values[k:k + 1]
+        return [total[:, p * LANES:(p + 1) * LANES] for p in range(width // LANES)]
+
+    def plane_out(src, frame, time_band, previous):
         for copy in previous:
             copy.wait()
-
-        def halo():
-            send_edge(slot, src).wait_recv()
-            return panels_of(edges.at[slot], width)(0, HALO)
-
-        first_columns(panels_of(src, width), halo, upper, w_ref, one)
+        first_columns(panels_of(src, width), lambda: halo_of(src), upper, w_ref, one)
         return rest_out(frame, time_band)
 
     def rest_out(frame, time_band):
@@ -372,7 +412,7 @@
 
     def second(c):
         r = rows(c)
-        send(0, 0, c, foot.at[0]).wait_recv()
+        send(0, 0, c, g).wait_recv()
         send(0, 1, c, g).wait_recv()
         f0, f2, first_o = f[0, r], f[2, r], o1[r]
         o_next = g[r] - 0.5 * jnp.where(last, f2, recv[0, 0, r])
@@ -384,15 +424,6 @@
         send(1, 0, c, s0).start()
         send(1, 1, c, h).start()
 
-        @pl.when(c == 0)
-        def _():
-            send_edge(1, o3).start()
-
-    each(second, 0, CHUNKS // 2)
-    copies, energy1 = plane_out(0, o1, 1, 0, [])
-    each(second, CHUNKS // 2)
-    copies, energy3 = plane_out(1, o3, 3, 0, copies)
-
     def third(c):
         r = rows(c)
         send(1, 0, c, s0).wait_recv()
@@ -415,16 +446,6 @@
             t0[r] = t - 0.5 * recv[2, 1, r]
             send(2, 1, c, t0).start()
 
-        @pl.when(c == 0)
-        def _():
-            send_edge(2, d2).start()
-
-    each(third)
-    copies, energy2 = plane_out(2, d2, 2, 1, copies)
-    for copy in copies:
-        copy.wait()
-    own_at, halo_at = strip_rows(one, upper)[1:]
-
     def fourth(c):
         r = rows(c)
         send(2, 0, c, t0).wait_recv()
@@ -441,25 +462,38 @@
             prev = jnp.where(first, after, recv[2, 1, r] - 0.5 * mine)
             top[r] = mine + 0.25 * (prev + after)
 
-        @pl.when(c == 0)
-        def _():
-            send_edge(3, top).start()
+    copies, energy1 = plane_out(o1, 1, 0, [])
+    each(second)
+    second(CHUNKS)
+    copies, energy3 = plane_out(o3, 3, 0, copies)
+    each(third)
+    third(CHUNKS)
+    copies, energy2 = plane_out(d2, 2, 1, copies)
+    for copy in copies:
+        copy.wait()
+    own_at, halo_at = strip_rows(one, upper)[1:]
+
+    def panels_at(r):
+        return [top[r, p * LANES:(p + 1) * LANES] for p in range(width // LANES)]
+
+    def finish(c):
+        fourth(c)
 
         def store(p, value):
-            one[p, pl.ds(pl.multiple_of(own_at + r.start, 8), size), :] = value
-
-        columns([top[r, p * LANES:(p + 1) * LANES] for p in range(width // LANES)], w_ref, 0, store)
-
-        @pl.when(c == CHUNKS - 2)
-        def _():
-            send_edge(3, top).wait_recv()
-
-            def store_halo(p, value):
-                one[p, pl.ds(halo_at, HALO), :] = value
-
-            columns(panels_of(edges.at[3], width)(0, HALO), w_ref, 0, store_halo)
-
-    each(fourth)
+            one[p, pl.ds(pl.multiple_of(own_at + c * size, 8), size), :] = value
+
+        columns(panels_at(rows(c)), w_ref, 0, store)
+
+    each(finish, 0, CHUNKS - 1)
+    fourth(CHUNKS - 1)
+    fourth(CHUNKS)
+
+    def store(p, value):
+        one[p, pl.ds(pl.multiple_of(own_at + strip - size, 8), size), :] = value[:size]
+        one[p, pl.ds(halo_at, HALO), :] = value[size:]
+
+    ends = [jnp.concatenate(pair, axis=0) for pair in zip(panels_at(rows(CHUNKS - 1)), halo_of(top))]
+    columns(ends, w_ref, 0, store)
     copies, energy0 = rest_out(0, jnp.where(odd, 2, 3))
     total = energy0 + energy1 + energy2 + energy3
 
@@ -498,11 +532,10 @@
             pl.when(slot != k)(lambda stage=stage, k=k: tell(stage, k).wait_send())
     for copy in copies:
         copy.wait()
-    for plane, src in enumerate((o1, o3, d2, top)):
-        send_edge(plane, src).wait_send()
+    exchange.wait_send()
 
     def drain(c):
-        send(0, 0, c, foot.at[0]).wait_send()
+        send(0, 0, c, g).wait_send()
         send(0, 1, c, g).wait_send()
         send(1, 0, c, s0).wait_send()
         send(1, 1, c, h).wait_send()
@@ -510,6 +543,7 @@
         send(2, 1, c, t0).wait_send()
 
     each(drain)
+    drain(CHUNKS)
 
 
 def spatial_scratch(strip, width):
@@ -522,7 +556,7 @@
 def shards(footage):
     frames, strip, width = footage.shape
     blocks = jnp.asarray(weight_blocks(width))
-    plane = pltpu.VMEM((strip, width), jnp.float32)
+    plane = pltpu.VMEM((strip + EXTRA, width), jnp.float32)
     dma = pltpu.SemaphoreType.DMA
     full = jax.ShapeDtypeStruct(footage.shape, jnp.float32)
     hbm = pl.BlockSpec(memory_space=pl.ANY)
@@ -532,20 +566,21 @@
     return pl.pallas_call(
         time_kernel,
         out_shape=(full, jax.ShapeDtypeStruct(size.shape, jnp.float32)),
-        in_specs=[hbm, vmem, vmem],
+        in_specs=[hbm, vmem, vmem, vmem],
         out_specs=(hbm, vmem),
         scratch_shapes=[
-            pltpu.VMEM(footage.shape, jnp.float32),
-            pltpu.VMEM((3, 2, strip, width), jnp.float32),
+            pltpu.VMEM((frames, strip + EXTRA, width), jnp.float32),
+            pltpu.VMEM((3, 2, strip + EXTRA, width), jnp.float32),
             *[plane] * 8,
-            pltpu.VMEM((4, HALO, width), jnp.float32),
+            pltpu.VMEM((frames, HALO, width), jnp.float32),
+            pltpu.VMEM((frames, EXTRA, width), jnp.float32),
             pltpu.VMEM((3, 2 * Y_CHIPS, 8, LANES), jnp.float32),
             *spatial_scratch(strip, width),
             dma((4,)),
-            dma((3, 2, CHUNKS)),
-            dma((3, 2, CHUNKS)),
-            dma((4,)),
-            dma((4,)),
+            dma,
+            dma((3, 2, CHUNKS + 1)),
+            dma((3, 2, CHUNKS + 1)),
+            dma((2,)),
             dma((width // LANES,)),
             dma((3, 2 * Y_CHIPS)),
             dma((3, 2 * Y_CHIPS)),
@@ -554,7 +589,7 @@
             collective_id=0, has_side_effects=True, vmem_limit_bytes=60 * 2**20
         ),
         name="time",
-    )(footage, blocks, jnp.asarray(size, jnp.float32))
+    )(footage, blocks, jnp.asarray(summaries()), jnp.asarray(size, jnp.float32))
 
 
 def solution(mesh):

time: 143 us -> 115 us (0.80)
  Pallas kernels: 131 us -> 105 us
    pallas_call x1, Pallas kernels: 131 us -> 105 us  [shards(): pl.pallas_call(time_kernel, out_shape=(full, jax.ShapeDtypeStruct(size.sh...]
where the time goes in v4:
time: 115 us; the launch traced here: 114 us
  Pallas kernels  105 us (91%)
  local copies, waits for them, and re-layouts  9.02 us (8%)
    pallas_call x1, Pallas kernels, shards(): pl.pallas_call(time_kernel, out_shape=(full, jax.ShapeDtypeStruct(size.sh...  105 us
    unnamed x4, local copies, waits for them, and re-layouts  9.02 us

profile of v4, /device:TPU:1, one launch (start us, length us, event | category | flops | bytes accessed | tf_op | source)
XLA Modules:
  0.0 114.3 jit_solution(17769270959625539397)
XLA Ops:
  0.6 104.6 %time.1 = (f32[4,512,1024]{2,1,0:T(8,128)}, f32[4,10]{1,0:T(4,128)}) custom-call(f32[4,512,1024]{2,1,0:T(8,128)} %foot.1, bf16[3,2,5,128,128]{4,3,2,1,0:T(8,128)(2,1)} %constant.6.clone.blocks_ref, f32[2,32,128]{2,1,0:T(8,128)} %constant.7.clone.basis_ref, f32[4,10]{1,0:T(4,128)} %constant.8.clone.counts_ref), custom_call_target="tpu_custom_call" | custom-call | tf_op jit(solution)/shard_map/time/pallas_call | solution.py:566
  105.3 0.0 copy-start
  105.3 8.4 %copy.8 = f32[4,512,1024]{2,1,0:T(8,128)} copy(f32[4,512,1024]{2,1,0:T(8,128)} %get-tuple-element.4) | data formatting | bytes 16777216
  113.7 0.0 copy-done
  113.7 0.6 copy.9
Async XLA Ops:
  105.3 8.5 %copy-start = (f32[4,10]{1,0:T(4,128)S(1)}, f32[4,10]{1,0:T(4,128)}, u32[]{:S(2)}) copy-start(f32[4,10]{1,0:T(4,128)} %get-tuple-element.5) | copy-start | bytes 484

commit v5 on v4

--- a/solution.py
+++ b/solution.py
@@ -150,7 +150,7 @@
         buf[p, ev, :] = buf[p, ev, :] * ZETA + (DELTA * ZETA * ZETA) * (buf[p, od_prev, :] + buf[p, od, :])
         return carry
 
-    lax.fori_loop(0, buf.shape[0], panel, 0)
+    lax.fori_loop(0, buf.shape[0], panel, 0, unroll=2)
 
 
 def strip_rows(one, upper):
@@ -205,7 +205,7 @@
         one[p, pl.ds(PAD, n, stride=2), :] = jnp.where(lane % 2 == 0, two[p, PAD:PAD + n, :], old)
         return carry
 
-    lax.fori_loop(0, panels, merge, 0)
+    lax.fori_loop(0, panels, merge, 0, unroll=2)
 
 
 def level_of(number, ceiling):
@@ -254,7 +254,7 @@
         value = one[p, pl.ds(at, strip), :]
         return acc + (value * value).reshape(-1, 8, LANES).sum(axis=0)
 
-    total = lax.fori_loop(0, panels, panel, jnp.zeros((8, LANES), jnp.float32))
+    total = lax.fori_loop(0, panels, panel, jnp.zeros((8, LANES), jnp.float32), unroll=2)
     bands = band_table((8, LANES))
     row = lax.broadcasted_iota(jnp.int32, (8, LANES), 0)
     col = lax.broadcasted_iota(jnp.int32, (8, LANES), 1)
@@ -319,9 +319,16 @@
     base = me - y_at
     groups = (
         (y_at, [(base + k, upper) for k in range(ring)]),
-        (x_at, [(me + (k - x_at) * 2 * ring, upper) for k in range(devices // (2 * ring))]),
-        (z_at + 2 * upper, [(me + (k % 2 - z_at) * ring, k // 2) for k in range(4)]),
+        (
+            x_at * 4 + z_at + 2 * upper,
+            [(me + (k // 4 - x_at) * 2 * ring + (k % 2 - z_at) * ring, k // 2 % 2) for k in range(4 * (devices // (2 * ring)))],
+        ),
     )
+
+    barrier = pltpu.get_barrier_semaphore()
+
+    def greet(where):
+        pl.semaphore_signal(barrier, inc=1, device_id=where, device_id_type=pl.DeviceIdType.MESH)
 
     border_at = pl.multiple_of((strip - HALO) * (1 - upper), HALO)
     borders = pltpu.make_async_copy(foot.at[:, pl.ds(border_at, HALO)], border, border_sem)
@@ -329,52 +336,47 @@
     loads = [pltpu.make_async_copy(foot.at[n], f.at[n, pl.ds(0, strip)], in_sem.at[n]) for n in range(4)]
     for n in (3, 2, 0, 1):
         loads[n].start()
-    barrier = pltpu.get_barrier_semaphore()
-
-    def greet(where):
-        pl.semaphore_signal(barrier, inc=1, device_id=where, device_id_type=pl.DeviceIdType.MESH)
-
+    for slot, members in groups[::-1]:
+        for k, where in enumerate(members):
+            pl.when(slot != k)(functools.partial(greet, where))
     for where in ((left, upper), (right, upper)):
         greet(where)
-    for slot, members in groups:
-        for k, where in enumerate(members):
-            pl.when(slot != k)(functools.partial(greet, where))
+
+    def partial(c):
+        r = rows(c)
+        g[r] = f[3, r] - 0.5 * f[2, r]
+
+    def first_high(c):
+        r = rows(c)
+        o1[r] = f[1, r] - 0.5 * (f[0, r] + f[2, r])
 
     borders.wait()
     for n in range(4):
         values = border[n]
         for k in range(RANK):
             summary[n, k:k + 1, :] = (basis_ref[upper, :, k:k + 1] * values).sum(axis=0, keepdims=True)
-        summary[n, RANK:, :] = jnp.zeros((EXTRA - RANK, width), jnp.float32)
+        f[n, strip + RANK:, :] = jnp.zeros((EXTRA - RANK, width), jnp.float32)
     exchange = pltpu.make_async_remote_copy(
-        src_ref=summary,
-        dst_ref=f.at[:, pl.ds(strip, EXTRA)],
+        src_ref=summary.at[:, pl.ds(0, RANK)],
+        dst_ref=f.at[:, pl.ds(strip, RANK)],
         send_sem=across.at[0],
         recv_sem=across.at[1],
         device_id=(me, 1 - upper),
         device_id_type=pl.DeviceIdType.MESH,
     )
-    pl.semaphore_wait(barrier, 2 + sum(len(members) - 1 for _, members in groups))
-    exchange.start()
-
-    def first_left():
-        each(lambda c: send(0, 0, c, foot.at[0]).start())
-
-    def first_right():
-        each(lambda c: send(0, 1, c, g).start())
-
-    def partial(c):
-        r = rows(c)
-        g[r] = f[3, r] - 0.5 * f[2, r]
-
-    def first_high(c):
-        r = rows(c)
-        o1[r] = f[1, r] - 0.5 * (f[0, r] + f[2, r])
-
-    pl.when(y_at != 0)(first_left)
     loads[3].wait()
     loads[2].wait()
     each(partial)
+    pl.semaphore_wait(barrier, 2 + sum(len(members) - 1 for _, members in groups))
+    exchange.start()
+
+    def first_left():
+        each(lambda c: send(0, 0, c, foot.at[0]).start())
+
+    def first_right():
+        each(lambda c: send(0, 1, c, g).start())
+
+    pl.when(y_at != 0)(first_left)
     pl.when(y_at != ring - 1)(first_right)
     loads[0].wait()
     loads[1].wait()
@@ -546,6 +548,31 @@
     drain(CHUNKS)
 
 
+def copy_kernel(src, energy_in, out, energy_out, stage, small, sems, small_sems):
+    parts = stage.shape[0]
+    frames, strip = src.shape[:2]
+    size = frames * strip // parts
+
+    def ends(k):
+        at = pl.ds(k * size % strip, size)
+        take = pltpu.make_async_copy(src.at[k * size // strip, at], stage.at[k], sems.at[0, k])
+        put = pltpu.make_async_copy(stage.at[k], out.at[k * size // strip, at], sems.at[1, k])
+        return take, put
+
+    copies = [ends(k) for k in range(parts)]
+    copies.append((
+        pltpu.make_async_copy(energy_in, small, small_sems.at[0]),
+        pltpu.make_async_copy(small, energy_out, small_sems.at[1]),
+    ))
+    for take, _ in copies:
+        take.start()
+    for take, put in copies:
+        take.wait()
+        put.start()
+    for _, put in copies:
+        put.wait()
+
+
 def spatial_scratch(strip, width):
     panels, rows = width // LANES, strip + HALO
     return [pltpu.VMEM((SLEVELS, 2, 3, 4 * LANES, 2 * LANES), jnp.bfloat16)] + [
@@ -563,7 +590,7 @@
     vmem = pl.BlockSpec(memory_space=pltpu.VMEM)
     devices = lax.axis_size("frame")
     size = counts(frames * devices, strip * lax.axis_size("row"), width)
-    return pl.pallas_call(
+    coeffs, energies = pl.pallas_call(
         time_kernel,
         out_shape=(full, jax.ShapeDtypeStruct(size.shape, jnp.float32)),
         in_specs=[hbm, vmem, vmem, vmem],
@@ -574,7 +601,7 @@
             *[plane] * 8,
             pltpu.VMEM((frames, HALO, width), jnp.float32),
             pltpu.VMEM((frames, EXTRA, width), jnp.float32),
-            pltpu.VMEM((3, 2 * Y_CHIPS, 8, LANES), jnp.float32),
+            pltpu.VMEM((2, 4 * Y_CHIPS, 8, LANES), jnp.float32),
             *spatial_scratch(strip, width),
             dma((4,)),
             dma,
@@ -582,14 +609,29 @@
             dma((3, 2, CHUNKS + 1)),
             dma((2,)),
             dma((width // LANES,)),
-            dma((3, 2 * Y_CHIPS)),
-            dma((3, 2 * Y_CHIPS)),
+            dma((2, 4 * Y_CHIPS)),
+            dma((2, 4 * Y_CHIPS)),
         ],
         compiler_params=pltpu.CompilerParams(
             collective_id=0, has_side_effects=True, vmem_limit_bytes=60 * 2**20
         ),
         name="time",
     )(footage, blocks, jnp.asarray(summaries()), jnp.asarray(size, jnp.float32))
+    parts = 16
+    return pl.pallas_call(
+        copy_kernel,
+        out_shape=(full, jax.ShapeDtypeStruct(size.shape, jnp.float32)),
+        in_specs=[hbm, hbm],
+        out_specs=(hbm, hbm),
+        scratch_shapes=[
+            pltpu.VMEM((parts, frames * strip // parts, width), jnp.float32),
+            pltpu.VMEM(size.shape, jnp.float32),
+            dma((2, parts)),
+            dma((2,)),
+        ],
+        compiler_params=pltpu.CompilerParams(vmem_limit_bytes=60 * 2**20),
+        name="copy_out",
+    )(coeffs, energies)
 
 
 def solution(mesh):

time: 115 us -> 110 us (0.957)
  local copies, waits for them, and re-layouts: 9.02 us -> 0 us
  Pallas kernels: 105 us -> 109 us
    unnamed x4 -> x0, local copies, waits for them, and re-layouts: 9.02 us -> none
    pallas_call x0 -> x1, Pallas kernels: none -> 6.59 us  [shards(): pl.pallas_call(copy_kernel, out_shape=(full, jax.ShapeDtypeStruct(size.sh...]
    pallas_call x1, Pallas kernels: 105 us -> 102 us  [shards(): pl.pallas_call(time_kernel, out_shape=(full, jax.ShapeDtypeStruct(size.sh...]
where the time goes in v5:
time: 110 us
  Pallas kernels  109 us (99%)
    pallas_call x1, Pallas kernels, shards(): pl.pallas_call(time_kernel, out_shape=(full, jax.ShapeDtypeStruct(size.sh...  102 us
    pallas_call x1, Pallas kernels, shards(): pl.pallas_call(copy_kernel, out_shape=(full, jax.ShapeDtypeStruct(size.sh...  6.59 us

profile of v5, /device:TPU:1, one launch (start us, length us, event | category | flops | bytes accessed | tf_op | source)
XLA Modules:
  0.0 109.7 jit_solution(6512049897807022582)
XLA Ops:
  0.6 102.3 %time.1 = (f32[4,512,1024]{2,1,0:T(8,128)}, f32[4,10]{1,0:T(4,128)}) custom-call(f32[4,512,1024]{2,1,0:T(8,128)} %foot.1, bf16[3,2,5,128,128]{4,3,2,1,0:T(8,128)(2,1)} %constant.6.clone.blocks_ref, f32[2,32,128]{2,1,0:T(8,128)} %constant.7.clone.basis_ref, f32[4,10]{1,0:T(4,128)} %constant.8.clone.counts_ref), custom_call_target="tpu_custom_call" | custom-call | tf_op jit(solution)/shard_map/time/pallas_call | solution.py:593
  102.9 6.6 %copy_out.1 = (f32[4,512,1024]{2,1,0:T(8,128)}, f32[4,10]{1,0:T(4,128)}) custom-call(f32[4,512,1024]{2,1,0:T(8,128)} %get-tuple-element.4.src, f32[4,10]{1,0:T(4,128)} %get-tuple-element.5.energy_in), custom_call_target="tpu_custom_call" | custom-call | tf_op jit(solution)/shard_map/copy_out/pallas_call | solution.py:621

commit v6 on v5

--- a/solution.py
+++ b/solution.py
@@ -247,20 +247,21 @@
     return float(frames) * rows * cols * np.outer(share, table)
 
 
-def band_energy(one, at, strip, time_band):
-    panels = one.shape[0]
-
+def square_rows(one, at, n):
     def panel(p, acc):
-        value = one[p, pl.ds(at, strip), :]
+        value = one[p, pl.ds(at, n), :]
         return acc + (value * value).reshape(-1, 8, LANES).sum(axis=0)
 
-    total = lax.fori_loop(0, panels, panel, jnp.zeros((8, LANES), jnp.float32), unroll=2)
+    return lax.fori_loop(0, one.shape[0], panel, jnp.zeros((8, LANES), jnp.float32), unroll=2)
+
+
+def band_energy(total, time_band):
     bands = band_table((8, LANES))
     row = lax.broadcasted_iota(jnp.int32, (8, LANES), 0)
     col = lax.broadcasted_iota(jnp.int32, (8, LANES), 1)
     acc = jnp.zeros((8, LANES), jnp.float32)
     for s in range(3 * SLEVELS + 1):
-        part = jnp.sum(jnp.where(bands == s, total, 0.0))
+        part = jnp.sum(jnp.where(bands == s, total, 0.0), axis=1, keepdims=True).sum(axis=0, keepdims=True)
         acc = acc + jnp.where((row == time_band) & (col == s), part, 0.0)
     return acc
 
@@ -271,10 +272,10 @@
     return own
 
 
-def put_strip(one, at, strip, out_plane, sem):
+def put_rows(one, at, n, out_plane, to, sem):
     return [
         pltpu.make_async_copy(
-            one.at[p, pl.ds(at, strip)], out_plane.at[:, p * LANES:(p + 1) * LANES], sem.at[p]
+            one.at[p, pl.ds(at, n)], out_plane.at[pl.ds(to, n), p * LANES:(p + 1) * LANES], sem.at[p]
         )
         for p in range(one.shape[0])
     ]
@@ -282,9 +283,11 @@
 
 def time_kernel(
     foot, blocks_ref, basis_ref, counts_ref, out, energy_ref,
-    f, recv, g, o1, o3, s0, h, d2, t0, top, border, summary, shared, w_ref, one, two, three,
-    in_sem, border_sem, send_sem, recv_sem, across, out_sem, sum_send, sum_recv,
+    f, recv, g, o1, o3, s0, h, d2, t0, top, border, summary, shared, w_ref, *rest,
 ):
+    bufs, far_bufs, near_bufs = rest[0:3], rest[3:6], rest[6:9]
+    one = bufs[0]
+    in_sem, border_sem, send_sem, recv_sem, across, out_sem, sum_send, sum_recv = rest[9:]
     strip, width = foot.shape[1:]
     me, upper = lax.axis_index("frame"), lax.axis_index("row")
     devices = lax.axis_size("frame")
@@ -296,7 +299,8 @@
     def rows(c):
         if isinstance(c, int) and c == CHUNKS:
             return pl.ds(strip, EXTRA)
-        return pl.ds(pl.multiple_of(c * size, size), size)
+        at = jnp.where(upper == 0, c, CHUNKS - 1 - c) * size
+        return pl.ds(pl.multiple_of(at, size), size)
 
     def send(level, side, c, src):
         return pltpu.make_async_remote_copy(
@@ -389,8 +393,6 @@
     send(0, 0, CHUNKS, f.at[0]).start()
     send(0, 1, CHUNKS, g).start()
     build_weights(blocks_ref, w_ref)
-    bufs = (one, two, three)
-
     def halo_of(src):
         values = src[rows(CHUNKS)]
         total = basis_ref[1 - upper, :, 0:1] * values[0:1]
@@ -402,15 +404,12 @@
         for copy in previous:
             copy.wait()
         first_columns(panels_of(src, width), lambda: halo_of(src), upper, w_ref, one)
-        return rest_out(frame, time_band)
-
-    def rest_out(frame, time_band):
         after_first_columns(w_ref, bufs)
         own_at = strip_rows(one, upper)[1]
-        copies = put_strip(one, own_at, strip, out.at[frame], out_sem)
+        copies = put_rows(one, own_at, strip, out.at[frame], 0, out_sem.at[0])
         for copy in copies:
             copy.start()
-        return copies, band_energy(one, own_at, strip, time_band)
+        return copies, band_energy(square_rows(one, own_at, strip), time_band)
 
     def second(c):
         r = rows(c)
@@ -471,32 +470,58 @@
     each(third)
     third(CHUNKS)
     copies, energy2 = plane_out(d2, 2, 1, copies)
-    for copy in copies:
-        copy.wait()
-    own_at, halo_at = strip_rows(one, upper)[1:]
-
-    def panels_at(r):
-        return [top[r, p * LANES:(p + 1) * LANES] for p in range(width // LANES)]
-
-    def finish(c):
+
+    far = CHUNKS - 2
+    far_base = (strip - far * size) * upper
+    near_shift = jnp.where(upper == 0, -(far - 1) * size, HALO)
+    near_halo = 3 * size * (1 - upper)
+
+    def into(buf, at, n):
+        return buf, pl.ds(pl.multiple_of(PAD + at, 8), n)
+
+    def finish(c, targets, halo=None):
+        values = [top[rows(c), p * LANES:(p + 1) * LANES] for p in range(width // LANES)]
+        if halo is not None:
+            values = [jnp.concatenate(pair, axis=0) for pair in zip(values, halo)]
+
+        def store(p, value):
+            for (buf, r), begin in targets:
+                buf[p, r, :] = value[begin:begin + r.size]
+
+        columns(values, w_ref, 0, store)
+
+    def finish_far(c):
         fourth(c)
-
-        def store(p, value):
-            one[p, pl.ds(pl.multiple_of(own_at + c * size, 8), size), :] = value
-
-        columns(panels_at(rows(c)), w_ref, 0, store)
-
-    each(finish, 0, CHUNKS - 1)
+        finish(c, [(into(far_bufs[0], rows(c).start - far_base, size), 0)])
+
+    each(finish_far, 0, far - 1)
+    at = rows(far - 1).start
+    fourth(far - 1)
+    finish(far - 1, [(into(far_bufs[0], at - far_base, size), 0), (into(near_bufs[0], at + near_shift, size), 0)])
+    after_first_columns(w_ref, far_bufs)
+    far_rows = far * size - HALO
+    far_at = pl.multiple_of(PAD + HALO * upper, 8)
+    far_to = pl.multiple_of((strip - far_rows) * upper, 8)
+    far_copies = put_rows(far_bufs[0], far_at, far_rows, out.at[0], far_to, out_sem.at[1])
+    for copy in far_copies:
+        copy.start()
+    squares = square_rows(far_bufs[0], far_at, far_rows)
+
+    fourth(CHUNKS - 2)
+    finish(CHUNKS - 2, [(into(near_bufs[0], rows(CHUNKS - 2).start + near_shift, size), 0)])
     fourth(CHUNKS - 1)
     fourth(CHUNKS)
-
-    def store(p, value):
-        one[p, pl.ds(pl.multiple_of(own_at + strip - size, 8), size), :] = value[:size]
-        one[p, pl.ds(halo_at, HALO), :] = value[size:]
-
-    ends = [jnp.concatenate(pair, axis=0) for pair in zip(panels_at(rows(CHUNKS - 1)), halo_of(top))]
-    columns(ends, w_ref, 0, store)
-    copies, energy0 = rest_out(0, jnp.where(odd, 2, 3))
+    near_last = into(near_bufs[0], rows(CHUNKS - 1).start + near_shift, size)
+    finish(CHUNKS - 1, [(near_last, 0), (into(near_bufs[0], near_halo, HALO), size)], halo_of(top))
+    after_first_columns(w_ref, near_bufs)
+    near_rows = strip - far_rows
+    near_to = pl.multiple_of(far_rows * (1 - upper), 8)
+    near_copies = put_rows(near_bufs[0], PAD + HALO, near_rows, out.at[0], near_to, out_sem.at[2])
+    for copy in near_copies:
+        copy.start()
+    squares = squares + square_rows(near_bufs[0], PAD + HALO, near_rows)
+    copies = copies + far_copies + near_copies
+    energy0 = band_energy(squares, jnp.where(odd, 2, 3))
     total = energy0 + energy1 + energy2 + energy3
 
     def tell(stage, k):
@@ -573,11 +598,8 @@
         put.wait()
 
 
-def spatial_scratch(strip, width):
-    panels, rows = width // LANES, strip + HALO
-    return [pltpu.VMEM((SLEVELS, 2, 3, 4 * LANES, 2 * LANES), jnp.bfloat16)] + [
-        pltpu.VMEM((panels, rows // k + 2 * PAD, LANES), jnp.float32) for k in (1, 2, 4)
-    ]
+def row_buffers(rows, width):
+    return [pltpu.VMEM((width // LANES, rows // k + 2 * PAD, LANES), jnp.float32) for k in (1, 2, 4)]
 
 
 def shards(footage):
@@ -602,13 +624,16 @@
             pltpu.VMEM((frames, HALO, width), jnp.float32),
             pltpu.VMEM((frames, EXTRA, width), jnp.float32),
             pltpu.VMEM((2, 4 * Y_CHIPS, 8, LANES), jnp.float32),
-            *spatial_scratch(strip, width),
+            pltpu.VMEM((SLEVELS, 2, 3, 4 * LANES, 2 * LANES), jnp.bfloat16),
+            *row_buffers(strip + HALO, width),
+            *row_buffers((CHUNKS - 2) * (strip // CHUNKS), width),
+            *row_buffers(3 * (strip // CHUNKS) + HALO, width),
             dma((4,)),
             dma,
             dma((3, 2, CHUNKS + 1)),
             dma((3, 2, CHUNKS + 1)),
             dma((2,)),
-            dma((width // LANES,)),
+            dma((3, width // LANES)),
             dma((2, 4 * Y_CHIPS)),
             dma((2, 4 * Y_CHIPS)),
         ],

time: 110 us -> 108 us (0.982)
  Pallas kernels: 109 us -> 107 us
    pallas_call x1, Pallas kernels: 102 us -> 101 us  [shards(): pl.pallas_call(time_kernel, out_shape=(full, jax.ShapeDtypeStruct(size.sh...]
where the time goes in v6:
time: 108 us
  Pallas kernels  107 us (99%)
    pallas_call x1, Pallas kernels, shards(): pl.pallas_call(time_kernel, out_shape=(full, jax.ShapeDtypeStruct(size.sh...  101 us
    pallas_call x1, Pallas kernels, shards(): pl.pallas_call(copy_kernel, out_shape=(full, jax.ShapeDtypeStruct(size.sh...  6.59 us

profile of v6, /device:TPU:1, one launch (start us, length us, event | category | flops | bytes accessed | tf_op | source)
XLA Modules:
  0.0 108.2 jit_solution(266910409029509270)
XLA Ops:
  0.6 100.8 %time.1 = (f32[4,512,1024]{2,1,0:T(8,128)}, f32[4,10]{1,0:T(4,128)}) custom-call(f32[4,512,1024]{2,1,0:T(8,128)} %foot.1, bf16[3,2,5,128,128]{4,3,2,1,0:T(8,128)(2,1)} %constant.6.clone.blocks_ref, f32[2,32,128]{2,1,0:T(8,128)} %constant.7.clone.basis_ref, f32[4,10]{1,0:T(4,128)} %constant.8.clone.counts_ref), custom_call_target="tpu_custom_call" | custom-call | tf_op jit(solution)/shard_map/time/pallas_call | solution.py:615
  101.4 6.6 %copy_out.1 = (f32[4,512,1024]{2,1,0:T(8,128)}, f32[4,10]{1,0:T(4,128)}) custom-call(f32[4,512,1024]{2,1,0:T(8,128)} %get-tuple-element.4.src, f32[4,10]{1,0:T(4,128)} %get-tuple-element.5.energy_in), custom_call_target="tpu_custom_call" | custom-call | tf_op jit(solution)/shard_map/copy_out/pallas_call | solution.py:646

commit v7 on v6

--- a/solution.py
+++ b/solution.py
@@ -154,7 +154,7 @@
 
 
 def strip_rows(one, upper):
-    strip = one.shape[1] - 2 * PAD - HALO
+    strip = one.shape[1] - 3 * PAD - HALO
     own_at = pl.multiple_of(PAD + HALO * upper, 8)
     halo_at = pl.multiple_of(PAD + strip * (1 - upper), 8)
     return strip, own_at, halo_at
@@ -179,7 +179,7 @@
 def after_first_columns(w_ref, bufs):
     one, two, three = bufs
     panels = one.shape[0]
-    rows = one.shape[1] - 2 * PAD
+    rows = one.shape[1] - 3 * PAD
     lift_rows(one, rows // 2)
 
     def into(buf, n):
@@ -599,7 +599,7 @@
 
 
 def row_buffers(rows, width):
-    return [pltpu.VMEM((width // LANES, rows // k + 2 * PAD, LANES), jnp.float32) for k in (1, 2, 4)]
+    return [pltpu.VMEM((width // LANES, rows // k + 3 * PAD, LANES), jnp.float32) for k in (1, 2, 4)]
 
 
 def shards(footage):

time: 108 us -> 108 us (level)
  no operation moved by 1% of the time
where the time goes in v7:
time: 108 us
  Pallas kernels  107 us (99%)
    pallas_call x1, Pallas kernels, shards(): pl.pallas_call(time_kernel, out_shape=(full, jax.ShapeDtypeStruct(size.sh...  101 us
    pallas_call x1, Pallas kernels, shards(): pl.pallas_call(copy_kernel, out_shape=(full, jax.ShapeDtypeStruct(size.sh...  6.59 us

profile of v7, /device:TPU:1, one launch (start us, length us, event | category | flops | bytes accessed | tf_op | source)
XLA Modules:
  0.0 108.1 jit_solution(18103174313863269868)
XLA Ops:
  0.6 100.8 %time.1 = (f32[4,512,1024]{2,1,0:T(8,128)}, f32[4,10]{1,0:T(4,128)}) custom-call(f32[4,512,1024]{2,1,0:T(8,128)} %foot.1, bf16[3,2,5,128,128]{4,3,2,1,0:T(8,128)(2,1)} %constant.6.clone.blocks_ref, f32[2,32,128]{2,1,0:T(8,128)} %constant.7.clone.basis_ref, f32[4,10]{1,0:T(4,128)} %constant.8.clone.counts_ref), custom_call_target="tpu_custom_call" | custom-call | tf_op jit(solution)/shard_map/time/pallas_call | solution.py:615
  101.4 6.6 %copy_out.1 = (f32[4,512,1024]{2,1,0:T(8,128)}, f32[4,10]{1,0:T(4,128)}) custom-call(f32[4,512,1024]{2,1,0:T(8,128)} %get-tuple-element.4.src, f32[4,10]{1,0:T(4,128)} %get-tuple-element.5.energy_in), custom_call_target="tpu_custom_call" | custom-call | tf_op jit(solution)/shard_map/copy_out/pallas_call | solution.py:646
